TPU v7x, 16 devices: a whole 2x2x2 slice. The times are simulated.
16 devices in a mesh: dp: 2 (over z), tp: 8 (over y, x, core).
Axes of the slice: x: 2, y: 2, z: 2, core: 2. Of those that a mesh axis runs over, the one named last changes fastest.
Arguments:
- x: bfloat16 [16, 768, 4096], P('dp'), parts along dimension 0
- seq_lens: int32 [16], P('dp'), parts along dimension 0
- w_query: bfloat16 [4096, 4096], P(None, 'tp')
- w_key: bfloat16 [4096, 1024], P(None, 'tp')
- w_value: bfloat16 [4096, 1024], P(None, 'tp')
- w_out: bfloat16 [4096, 4096], P('tp')
- w_gate: bfloat16 [4096, 14336], P(None, 'tp')
- w_up: bfloat16 [4096, 14336], P(None, 'tp')
- w_down: bfloat16 [14336, 4096], P('tp')
- attn_gain: bfloat16 [4096], replicated
- mlp_gain: bfloat16 [4096], replicated
- k_cache: bfloat16 [16, 1536, 8, 128], P('dp', None, 'tp'), parts along dimension 0
- v_cache: bfloat16 [16, 1536, 8, 128], P('dp', None, 'tp'), parts along dimension 0
Outputs:
- output 1: bfloat16 [16, 768, 4096], P('dp'), parts along dimension 0
- output 2: bfloat16 [16, 1536, 8, 128], P('dp', None, 'tp'), parts along dimension 0
- output 3: bfloat16 [16, 1536, 8, 128], P('dp', None, 'tp'), parts along dimension 0
There are 2 independent parts. A program takes and returns all parts, laid end to end along the dimension named above; an argument that names none is the same for every part.
All inputs are finite; a program needn't handle non-finite values.
Results may differ from a plain program's by a relative error of at most 0.0114972.
Values are sent between devices in bfloat16 or wider.
A program may use at most 1 GiB of HBM per device.

v0:
```python
import jax
import jax.numpy as jnp
from jax import lax
from jax.sharding import PartitionSpec as P

EPS = 1e-5
ROPE_BASE = 10000.0


def rms_norm(rows, gain):
    rows32 = rows.astype(jnp.float32)
    inv_rms = lax.rsqrt(jnp.mean(rows32 * rows32, axis=-1, keepdims=True) + EPS)
    return (rows32 * inv_rms * gain.astype(jnp.float32)).astype(jnp.bfloat16)


def rotary(vecs):
    seq_len = vecs.shape[1]
    head_dim = vecs.shape[-1]
    half_dim = head_dim // 2
    inv_freq = ROPE_BASE ** (-jnp.arange(0, head_dim, 2).astype(jnp.float32) / head_dim)
    angles = jnp.arange(seq_len).astype(jnp.float32)[:, None] * inv_freq[None, :]
    table_shape = (1, seq_len) + (1,) * (vecs.ndim - 3) + (half_dim,)
    cos_tab = jnp.cos(angles).reshape(table_shape)
    sin_tab = jnp.sin(angles).reshape(table_shape)
    pairs = vecs.reshape(vecs.shape[:-1] + (half_dim, 2))
    even_part = pairs[..., 0]
    odd_part = pairs[..., 1]
    turned = jnp.stack([even_part * cos_tab - odd_part * sin_tab, even_part * sin_tab + odd_part * cos_tab], axis=-1)
    return turned.reshape(vecs.shape).astype(jnp.bfloat16)


def causal_attention(queries, keys, values, seq_lens):
    seq_len = queries.shape[1]
    head_dim = queries.shape[-1]
    scores = jnp.einsum("bqkgh,bskh->bkgqs", queries, keys, preferred_element_type=jnp.float32) * head_dim ** -0.5
    positions = jnp.arange(seq_len)
    allowed = (positions[None, None, :] <= positions[None, :, None]) & (positions[None, None, :] < seq_lens[:, None, None])
    scores = jnp.where(allowed[:, None, None], scores, -jnp.inf)
    probs = jax.nn.softmax(scores, axis=-1).astype(jnp.bfloat16)
    return jnp.einsum("bkgqs,bskh->bqkgh", probs, values, preferred_element_type=jnp.float32).astype(jnp.bfloat16)


def sum_partials(partial, resid_rows, tp_size):
    batch_size, seq_len, model_width = partial.shape
    stacked = partial.reshape(batch_size, tp_size, seq_len // tp_size, model_width)
    received = lax.all_to_all(stacked, "tp", 1, 1, tiled=True)
    summed = jnp.sum(received.astype(jnp.float32), axis=1)
    return (resid_rows.astype(jnp.float32) + summed).astype(jnp.bfloat16)


def solution(mesh):
    tp_size = mesh.shape["tp"]

    def layer_shard(x, seq_lens, w_query, w_key, w_value, w_out, w_gate, w_up, w_down, attn_gain, mlp_gain, k_cache, v_cache):
        batch_size, seq_len, model_width = x.shape
        head_dim = k_cache.shape[3]
        kv_local = k_cache.shape[2]
        group_size = w_query.shape[1] // (head_dim * kv_local)
        rows_each = seq_len // tp_size
        tp_index = lax.axis_index("tp")
        normed = rms_norm(x, attn_gain)
        queries = rotary(jnp.einsum("bsd,dk->bsk", normed, w_query, preferred_element_type=jnp.float32).reshape(batch_size, seq_len, kv_local, group_size, head_dim))
        keys = rotary(jnp.einsum("bsd,dk->bsk", normed, w_key, preferred_element_type=jnp.float32).reshape(batch_size, seq_len, kv_local, head_dim))
        values = jnp.einsum("bsd,dk->bsk", normed, w_value, preferred_element_type=jnp.float32).astype(jnp.bfloat16).reshape(batch_size, seq_len, kv_local, head_dim)
        valid = (jnp.arange(seq_len)[None, :] < seq_lens[:, None])[:, :, None, None]
        keys = jnp.where(valid, keys, jnp.zeros_like(keys))
        values = jnp.where(valid, values, jnp.zeros_like(values))
        k_cache_out = lax.dynamic_update_slice(k_cache, keys, (0, 0, 0, 0))
        v_cache_out = lax.dynamic_update_slice(v_cache, values, (0, 0, 0, 0))
        attn_rows = causal_attention(queries, keys, values, seq_lens).reshape(batch_size, seq_len, -1)
        attn_part = jnp.einsum("bsk,kd->bsd", attn_rows, w_out, preferred_element_type=jnp.float32).astype(jnp.bfloat16)
        x_rows = lax.dynamic_slice_in_dim(x, tp_index * rows_each, rows_each, axis=1)
        hidden_rows = sum_partials(attn_part, x_rows, tp_size)
        normed_mlp = lax.all_gather(rms_norm(hidden_rows, mlp_gain), "tp", axis=1, tiled=True)
        gate_pre = jnp.einsum("bsd,df->bsf", normed_mlp, w_gate, preferred_element_type=jnp.float32)
        up_pre = jnp.einsum("bsd,df->bsf", normed_mlp, w_up, preferred_element_type=jnp.float32)
        gated = (jax.nn.silu(gate_pre) * up_pre).astype(jnp.bfloat16)
        mlp_part = jnp.einsum("bsf,fd->bsd", gated, w_down, preferred_element_type=jnp.float32).astype(jnp.bfloat16)
        out_rows = sum_partials(mlp_part, hidden_rows, tp_size)
        y = lax.all_gather(out_rows, "tp", axis=1, tiled=True)
        return y, k_cache_out, v_cache_out

    cache_spec = P("dp", None, "tp", None)
    return jax.shard_map(layer_shard, mesh=mesh, in_specs=(P("dp", None, None), P("dp"), P(None, "tp"), P(None, "tp"), P(None, "tp"), P("tp", None), P(None, "tp"), P(None, "tp"), P("tp", None), P(), P(), cache_spec, cache_spec), out_specs=(P("dp", None, None), cache_spec, cache_spec), check_vma=False)
```

profile of v0, /device:TPU:0, one launch (start us, length us, event | category | flops | bytes accessed | tf_op | source)
XLA Modules:
  0.0 2341.5 jit_solution(1864598468330433472)
XLA Ops:
  7.2 3.9 copy.77
  11.1 3.8 copy.76
  15.1 16.2 fusion
  31.3 23.2 fusion.9
  54.5 3.7 copy.65
  61.6 44.0 %fusion.7 = f32[8,768,512]{1,2,0:T(8,128)} fusion(bf16[8,768,4096]{2,1,0:T(8,128)(2,1)} %param.13, f32[4096]{0:T(1024)S(1)} %convert_element_type.129, f32[8,768]{1,0:T(8,128)S(1)} %add_rsqrt_fusion, bf16[4096,512]{1,0:T(8,128)(2,1)} %param.15), kind=kOutput, calls=%fused_computation.17 | convolution fusion | flops 25870467072 | bytes 67149824 | tf_op jit(solution)/shard_map/bsd,dk->bsk/dot_general | solution.py:62
  105.6 16.4 copy.66
  122.0 5.6 subtract_convert_fusion
  127.7 3.2 pad_maximum_fusion
  131.0 3.9 broadcast_and_fusion
  134.9 35.7 %fusion.4 = (f32[8,4,768]{2,1,0:T(4,128)S(1)}, f32[8,768,768,4]{2,1,3,0:T(8,128)}) fusion(pred[8,768,768]{1,2,0:T(8,128)(4,1)} %broadcast_and_fusion, bf16[8,768,4,128]{1,0,3,2:T(8,128)(2,1)} %bitcast.81, bf16[8,768,128]{2,1,0:T(8,128)(2,1)S(1)} %copy-done.7, pred[8,768]{1,0:T(8,128)(4,1)S(1)} %iota_compare_fusion.1), kind=kOutput, calls=%fused_computation.11 | convolution fusion | flops 4889223168 | bytes 88184832 | tf_op jit(solution)/shard_map/bqkgh,bskh->bkgqs/dot_general | solution.py:35
  170.6 25.4 %fusion.3 = f32[8,4,768]{2,1,0:T(4,128)S(1)} fusion(f32[8,768,768,4]{2,1,3,0:T(8,128)} %get-tuple-element.12, f32[8,4,768]{2,1,0:T(4,128)S(1)} %get-tuple-element.11, pred[8,768,768]{1,2,0:T(8,128)(4,1)} %broadcast_and_fusion), kind=kLoop, calls=%fused_computation.10 | loop fusion | flops 75472896 | bytes 80412672 | tf_op jit(solution)/shard_map/reduce_sum | solution.py:39
  196.0 23.1 bitcast_dynamic-update-slice_fusion
  219.1 31.9 %fusion.25 = bf16[8,128,4,768]{3,1,2,0:T(8,128)(2,1)} fusion(f32[8,4,768]{2,1,0:T(4,128)S(1)} %fusion.3, f32[8,4,768]{2,1,0:T(4,128)S(1)} %get-tuple-element.11, f32[8,768,768,4]{2,1,3,0:T(8,128)} %get-tuple-element.12, pred[8,768,768]{1,2,0:T(8,128)(4,1)} %broadcast_and_fusion, bf16[8,768,128]{2,1,0:T(8,128)(2,1)} %get-tuple-element.14), kind=kOutput, calls=%fused_computation.40 | convolution fusion | flops 4929355776 | bytes 88276992 | tf_op jit(solution)/shard_map/bkgqs,bskh->bqkgh/dot_general | solution.py:40
  250.9 34.5 %convolution_convert_fusion.1 = bf16[8,768,4096]{2,1,0:T(8,128)(2,1)} fusion(bf16[8,768,512]{1,2,0:T(8,128)(2,1)} %bitcast.82, bf16[512,4096]{1,0:T(8,128)(2,1)} %param.18), kind=kOutput, calls=%fused_computation.16 | convolution fusion | flops 25794969600 | bytes 60817408 | tf_op jit(solution)/shard_map/bsk,kd->bsd/dot_general | solution.py:71
  285.4 33.7 %copy.51 = bf16[8,8,96,4096]{3,2,0,1:T(8,128)(2,1)} copy(bf16[8,8,96,4096]{3,2,1,0:T(8,128)(2,1)} %bitcast.75) | data formatting | bytes 100663296 | tf_op jit(solution)/shard_map/reshape | solution.py:45
  319.2 8.7 all-to-all-start
  327.9 544.7 %all-to-all-done = bf16[8,8,96,4096]{3,2,0,1:T(8,128)(2,1)} async-done(((bf16[8,8,96,4096]{3,2,0,1:T(8,128)(2,1)}), bf16[8,8,96,4096]{3,2,0,1:T(8,128)(2,1)}, u32[]{:S(2)}, u32[]{:S(2)}) %all-to-all-start) | async-done | bytes 50331680 | tf_op jit(solution)/shard_map/all_to_all | solution.py:46
  872.6 21.8 convert_reduce_fusion.1
  894.3 7.4 fusion.17
  901.8 2.6 copy-done.2
  904.4 5.4 fusion.19
  909.9 228.7 %all-gather.3.cloned.1.call-done = bf16[8,768,4096]{2,1,0:T(8,128)(2,1)} async-done(((bf16[8,96,4096]{2,1,0:T(8,128)(2,1)}), bf16[8,768,4096]{2,1,0:T(8,128)(2,1)}) %all-gather.3.cloned.1.call-update) | async-done | bytes 50331664 | tf_op jit(solution)/shard_map/all_gather | solution.py:74
  1138.6 102.3 %fusion.14 = f32[8,768,1792]{2,1,0:T(8,128)} fusion(bf16[8,768,4096]{2,1,0:T(8,128)(2,1)} %all-gather.3.cloned.1.call-done, bf16[4096,1792]{1,0:T(8,128)(2,1)} %param.20), kind=kOutput, calls=%fused_computation.24 | convolution fusion | flops 90194313216 | bytes 109051904 | tf_op jit(solution)/shard_map/bsd,df->bsf/dot_general | solution.py:76
  1240.9 106.6 %multiply_convert_fusion = bf16[8,768,1792]{2,1,0:T(8,128)(2,1)} fusion(f32[8,768,1792]{2,1,0:T(8,128)} %fusion.14, bf16[8,768,4096]{2,1,0:T(8,128)(2,1)} %all-gather.3.cloned.1.call-done, bf16[4096,1792]{1,0:T(8,128)(2,1)} %param.19), kind=kOutput, calls=%fused_computation.12 | convolution fusion | flops 90260373504 | bytes 131072000 | tf_op jit(solution)/shard_map/bsd,df->bsf/dot_general | solution.py:75
  1347.5 100.7 %convolution_convert_fusion = bf16[8,768,4096]{2,1,0:T(8,128)(2,1)} fusion(bf16[8,768,1792]{2,1,0:T(8,128)(2,1)} %multiply_convert_fusion, bf16[1792,4096]{1,0:T(8,128)(2,1)} %param.21), kind=kOutput, calls=%fused_computation.15 | convolution fusion | flops 90219479040 | bytes 87031808 | tf_op jit(solution)/shard_map/bsf,fd->bsd/dot_general | solution.py:78
  1448.2 33.8 %copy.52 = bf16[8,8,96,4096]{3,2,0,1:T(8,128)(2,1)} copy(bf16[8,8,96,4096]{3,2,1,0:T(8,128)(2,1)} %bitcast.76) | data formatting | bytes 100663296 | tf_op jit(solution)/shard_map/reshape | solution.py:45
  1482.0 558.0 %all_to_all.10 = bf16[8,8,96,4096]{3,2,0,1:T(8,128)(2,1)} all-to-all(bf16[8,8,96,4096]{3,2,0,1:T(8,128)(2,1)} %copy.52), channel_id=1, replica_groups=mesh['dp'=2,'tp'=8] {'tp'}, dimensions={1} | all-to-all | bytes 100663296 | tf_op jit(solution)/shard_map/all_to_all | solution.py:46
  2040.0 21.5 convert_reduce_fusion
  2061.5 11.5 fusion.20
  2077.8 222.7 %all-gather.5.cloned.1.call-done = bf16[8,768,4096]{2,1,0:T(8,128)(2,1)} async-done(((bf16[8,96,4096]{2,1,0:T(8,128)(2,1)}), bf16[8,768,4096]{2,1,0:T(8,128)(2,1)}) %all-gather.5.cloned.1.call-update) | async-done | bytes 50331664 | tf_op jit(solution)/shard_map/all_gather | solution.py:80
  2300.5 33.8 %copy.78 = bf16[8,768,4096]{2,1,0:T(8,128)(2,1)} copy(bf16[8,768,4096]{2,1,0:T(8,128)(2,1)} %all-gather.5.cloned.1.call-done) | data formatting | bytes 100663296
  (46 shorter events, 8.6 us)
Async XLA Ops:
  7.2 188.8 %copy-start = (bf16[4096,128]{1,0:T(8,128)(2,1)S(1)}, bf16[4096,128]{1,0:T(8,128)(2,1)}, u32[]{:S(2)}) copy-start(bf16[4096,128]{1,0:T(8,128)(2,1)} %param.17) | copy-start | bytes 3145732
  15.0 16.3 copy-start.10
  15.0 16.3 copy-start.13
  59.0 0.7 copy-start.5
  59.7 45.9 %copy-start.3 = (bf16[8,768,1,64,2]{1,0,4,3,2:T(8,128)(2,1)}, bf16[8,768,1,64,2]{1,0,4,3,2:T(8,128)(2,1)S(1)}, u32[]{:S(2)}) copy-start(bf16[8,768,1,64,2]{1,0,4,3,2:T(8,128)(2,1)S(1)} %maximum_convert_fusion) | copy-start | bytes 4718596
  105.6 16.4 copy-start.6
  122.0 5.6 copy-start.12
  127.7 7.2 copy-start.7
  127.7 68.2 %copy-start.8 = (pred[8,768]{1,0:T(8,128)(4,1)}, pred[8,768]{1,0:T(8,128)(4,1)S(1)}, u32[]{:S(2)}) copy-start(pred[8,768]{1,0:T(8,128)(4,1)S(1)} %iota_compare_fusion.1) | copy-start | bytes 18436
  319.2 8.7 copy-start.11
  319.2 553.4 %all-to-all-start = ((bf16[8,8,96,4096]{3,2,0,1:T(8,128)(2,1)}), bf16[8,8,96,4096]{3,2,0,1:T(8,128)(2,1)}, u32[]{:S(2)}, u32[]{:S(2)}) async-start(bf16[8,8,96,4096]{3,2,0,1:T(8,128)(2,1)} %copy.51), calls=%async_computation | async-start | bytes 100663296 | tf_op jit(solution)/shard_map/all_to_all | solution.py:46
  327.8 810.7 %all-gather.3.cloned.1.call-start = ((), (), s32[]{:S(2)}) async-start(), calls=%async_computation.2 | async-start | bytes 56623104 | tf_op jit(solution)/shard_map/all_gather | solution.py:74
  901.8 2.6 copy-start.2
  909.8 1390.7 %all-gather.5.cloned.1.call-start = ((), (), s32[]{:S(2)}) async-start(), calls=%async_computation.3 | async-start | bytes 56623104 | tf_op jit(solution)/shard_map/all_gather | solution.py:80
  2061.5 11.5 copy-start.4
  2061.5 11.5 copy-start.9
  2300.5 33.8 %copy-start.1 = (bf16[4096,128]{1,0:T(8,128)(2,1)S(1)}, bf16[4096,128]{1,0:T(8,128)(2,1)}, u32[]{:S(2)}) copy-start(bf16[4096,128]{1,0:T(8,128)(2,1)} %param.17) | copy-start | bytes 3145732
Sparse Core Ops, SparseCore 0:
  909.9 228.5 all-gather.2
  2073.2 227.3 all-gather.4
where the time goes:
time: 2350 us; the launch traced here: 2340 us
  waiting for transfers between devices  996 us (42%)
  blocking collectives  558 us (24%)
  matrix products  502 us (21%)
  local copies, waits for them, and re-layouts  137 us (6%)
  other arithmetic  125 us (5%)
    all_to_all x1, blocking collectives, sum_partials(): received = lax.all_to_all(stacked, 'tp', 1, 1, tiled=True)  558 us
    all_to_all x1, waiting for transfers between devices, sum_partials(): received = lax.all_to_all(stacked, 'tp', 1, 1, tiled=True)  545 us
    all_gather x1, waiting for transfers between devices, layer_shard(): lax.all_gather(rms_norm(hidden_rows, mlp_gain), 'tp', axis=1, tiled=True)  229 us
    all_gather x1, waiting for transfers between devices, layer_shard(): y = lax.all_gather(out_rows, 'tp', axis=1, tiled=True)  223 us
    dot_general x1, matrix products, layer_shard(): jnp.einsum('bsd,df->bsf', normed_mlp, w_gate, preferred_element_type=jnp....  107 us
    dot_general x1, matrix products, layer_shard(): jnp.einsum('bsd,df->bsf', normed_mlp, w_up, preferred_element_type=jnp.fl...  102 us
    dot_general x1, matrix products, layer_shard(): jnp.einsum('bsf,fd->bsd', gated, w_down, preferred_element_type=jnp.float32)  101 us
    reshape x2, local copies, waits for them, and re-layouts, sum_partials(): partial.reshape(batch_size, tp_size, seq_len // tp_size, model_width)  67.5 us
  transfers between devices with their start and end apart: 3, of which 3 were waited for; matrix products, arithmetic and copies ran while one was open for 0% of the time, Pallas kernels for 0%

commit v1 on v0

v1 whole, which is shorter than its diff:
```python
import functools

import jax
import jax.numpy as jnp
from jax import lax
from jax.experimental import pallas as pl
from jax.experimental.pallas import tpu as pltpu
from jax.sharding import PartitionSpec as P

EPS = 1e-5
ROPE_BASE = 10000.0
F32 = jnp.float32
BF16 = jnp.bfloat16
CHUNK = 2
TILE = 256


def rms_rows(rows, gain):
    rows32 = rows.astype(F32)
    inv_rms = lax.rsqrt(jnp.mean(rows32 * rows32, axis=-1, keepdims=True) + EPS)
    return (rows32 * inv_rms * gain.astype(F32)).astype(BF16)


def qkv_kernel(tiles, lens_ref, x_ref, gain_ref, wq_ref, wkv_ref, cos_ref, sin_ref, q_ref, k_ref, v_ref):
    step = pl.program_id(0)
    normed = rms_rows(x_ref[...], gain_ref[...])
    head = cos_ref.shape[1]
    cos_tab = cos_ref[...]
    sin_tab = sin_ref[...]
    even = lax.broadcasted_iota(jnp.int32, cos_tab.shape, 1) % 2 == 0

    def turn(part):
        swapped = jnp.where(even, pltpu.roll(part, head - 1, 1), pltpu.roll(part, 1, 1))
        return (part * cos_tab + swapped * sin_tab).astype(BF16)

    kv = jnp.dot(normed, wkv_ref[...], preferred_element_type=F32)
    rows = lax.rem(step, tiles) * cos_tab.shape[0] + lax.broadcasted_iota(jnp.int32, cos_tab.shape, 0)
    valid = rows < lens_ref[step // tiles]
    zero = jnp.zeros(cos_tab.shape, BF16)
    k_ref[...] = jnp.where(valid, turn(kv[:, :head]), zero)
    v_ref[...] = jnp.where(valid, kv[:, head:].astype(BF16), zero)
    queries = jnp.dot(normed, wq_ref[...], preferred_element_type=F32)
    for h in range(queries.shape[1] // head):
        cols = slice(h * head, (h + 1) * head)
        q_ref[:, cols] = turn(queries[:, cols])


def attention_kernel(first, lens_ref, q_ref, k_ref, v_ref, o_ref):
    length = lens_ref[first + pl.program_id(0)]
    seq_len, head = k_ref.shape
    scale = head ** -0.5
    for tile in range(seq_len // TILE):
        width = (tile + 1) * TILE
        rows = slice(tile * TILE, (tile + 1) * TILE)
        query_at = tile * TILE + lax.broadcasted_iota(jnp.int32, (TILE, width), 0)
        key_at = lax.broadcasted_iota(jnp.int32, (TILE, width), 1)
        allowed = (key_at <= query_at) & (key_at < length)
        for h in range(q_ref.shape[1] // head):
            cols = slice(h * head, (h + 1) * head)
            scores = lax.dot_general(q_ref[rows, cols], k_ref[:width, :], (((1,), (1,)), ((), ())), preferred_element_type=F32)
            scores = jnp.where(allowed, scores * scale, -jnp.inf)
            top = jnp.max(scores, axis=-1, keepdims=True)
            weights = jnp.exp(scores - top)
            probs = (weights / jnp.sum(weights, axis=-1, keepdims=True)).astype(BF16)
            o_ref[rows, cols] = jnp.dot(probs, v_ref[:width, :], preferred_element_type=F32).astype(BF16)


def out_kernel(core_ref, o_ref, w_ref, x_ref, gain_ref, h_ref, n_ref, total):
    step = pl.program_id(1)

    @pl.when(step == 0)
    def _():
        total[...] = jnp.zeros_like(total)

    part = jnp.dot(o_ref[0], w_ref[...], preferred_element_type=F32).astype(BF16)
    total[...] += part.astype(F32)

    @pl.when(step == pl.num_programs(1) - 1)
    def _():
        hidden = (x_ref[...].astype(F32) + total[...]).astype(BF16)
        h_ref[...] = hidden
        n_ref[...] = rms_rows(hidden, gain_ref[...])


def rope_tables(seq_len, head):
    inv_freq = ROPE_BASE ** (-jnp.arange(0, head, 2).astype(F32) / head)
    angles = jnp.arange(seq_len).astype(F32)[:, None] * inv_freq[None, :]
    sign = jnp.where(jnp.arange(head) % 2 == 0, -1.0, 1.0).astype(F32)
    return jnp.repeat(jnp.cos(angles), 2, axis=1), jnp.repeat(jnp.sin(angles), 2, axis=1) * sign


def vmem_limit(mib):
    return dict(vmem_limit_bytes=mib * 2 ** 20)


def project_qkv(x_rows, gain, w_query, w_kv, seq_lens, seq_len, head):
    rows, width = x_rows.shape
    tiles = seq_len // TILE
    cos_tab, sin_tab = rope_tables(seq_len, head)
    whole = lambda shape: pl.BlockSpec(shape, lambda i, s: (0, 0))
    table = pl.BlockSpec((TILE, head), lambda i, s: (lax.rem(i, tiles), 0))
    by_row = lambda cols: pl.BlockSpec((TILE, cols), lambda i, s: (i, 0))
    q_cols = w_query.shape[1]
    return pl.pallas_call(
        functools.partial(qkv_kernel, tiles),
        grid_spec=pltpu.PrefetchScalarGridSpec(
            num_scalar_prefetch=1, grid=(rows // TILE,),
            in_specs=[by_row(width), whole((1, width)), whole(w_query.shape), whole(w_kv.shape), table, table],
            out_specs=[by_row(q_cols), by_row(head), by_row(head)]),
        out_shape=[jax.ShapeDtypeStruct((rows, q_cols), BF16)] + [jax.ShapeDtypeStruct((rows, head), BF16)] * 2,
        compiler_params=pltpu.CompilerParams(**vmem_limit(56)),
        cost_estimate=pl.CostEstimate(flops=2 * rows * width * (q_cols + 2 * head), bytes_accessed=2 * rows * width, transcendentals=0),
    )(seq_lens, x_rows, gain.reshape(1, -1), w_query, w_kv, cos_tab, sin_tab)


def attend(queries, keys, values, seq_lens, first, count, seq_len):
    q_cols, head = queries.shape[1], keys.shape[1]
    by_seq = lambda cols: pl.BlockSpec((seq_len, cols), lambda i, s: (first + i, 0))
    return pl.pallas_call(
        functools.partial(attention_kernel, first),
        grid_spec=pltpu.PrefetchScalarGridSpec(
            num_scalar_prefetch=1, grid=(count,),
            in_specs=[by_seq(q_cols), by_seq(head), by_seq(head)],
            out_specs=pl.BlockSpec((seq_len, q_cols), lambda i, s: (i, 0))),
        out_shape=jax.ShapeDtypeStruct((count * seq_len, q_cols), BF16),
        compiler_params=pltpu.CompilerParams(**vmem_limit(48)),
        cost_estimate=pl.CostEstimate(flops=count * 8 * 10 ** 9, bytes_accessed=count * 2 * 10 ** 6, transcendentals=0),
    )(seq_lens, queries, keys, values)


def project_out(gathered, w_full, x_rows, gain, core, first, rows):
    groups, _, group_cols = gathered.shape
    width = w_full.shape[1]
    tile = rows // 2
    per = rows // tile
    row_block = pl.BlockSpec((tile, width), lambda r, i, c: (r, 0))
    return pl.pallas_call(
        out_kernel,
        grid_spec=pltpu.PrefetchScalarGridSpec(
            num_scalar_prefetch=1, grid=(per, groups),
            in_specs=[pl.BlockSpec((1, tile, group_cols), lambda r, i, c: (i, c[0] * per + r, 0)),
                      pl.BlockSpec((group_cols, width), lambda r, i, c: (i, 0)),
                      pl.BlockSpec((tile, width), lambda r, i, c: (first * per + c[0] * per + r, 0)),
                      pl.BlockSpec((1, width), lambda r, i, c: (0, 0))],
            out_specs=[row_block, row_block],
            scratch_shapes=[pltpu.VMEM((tile, width), F32)]),
        out_shape=[jax.ShapeDtypeStruct((rows, width), BF16)] * 2,
        compiler_params=pltpu.CompilerParams(**vmem_limit(56)),
        cost_estimate=pl.CostEstimate(flops=2 * rows * width * groups * group_cols, bytes_accessed=4 * width * width, transcendentals=0),
    )(core, gathered, w_full, x_rows, gain.reshape(1, -1))


def solution(mesh):
    tp_size = mesh.shape["tp"]
    sibling = [(i, i ^ 1) for i in range(tp_size)]
    first_axis = [(i, i ^ (4 if i % 2 else 2)) for i in range(tp_size)]
    second_axis = [(i, i ^ (2 if i % 2 else 4)) for i in range(tp_size)]
    swap = lambda value, pairs: lax.ppermute(value, "tp", pairs)

    def layer_shard(x, seq_lens, w_query, w_key, w_value, w_out, w_gate, w_up, w_down, attn_gain, mlp_gain, k_cache, v_cache):
        batch_size, seq_len, width = x.shape
        head = k_cache.shape[3]
        half = width // 2
        block = seq_len // 2
        me = lax.axis_index("tp")
        core = me % 2
        at_x = (me // 2) % 2
        at_y = me // 4
        bit_first = jnp.where(core == 0, at_x, at_y)
        bit_second = jnp.where(core == 0, at_y, at_x)
        pick = lambda value, index, axis=0: lax.dynamic_index_in_dim(value, index, axis, keepdims=False)

        w_full = lax.all_gather(w_out, "tp", axis=0, tiled=True)
        x_rows = x.reshape(batch_size * seq_len, width)
        queries, keys, values = project_qkv(x_rows, attn_gain, w_query, jnp.concatenate([w_key, w_value], axis=1), seq_lens, seq_len, head)
        as_cache = lambda rows: rows.reshape(batch_size, seq_len, 1, head)
        k_cache_out = lax.dynamic_update_slice(k_cache, as_cache(keys), (0, 0, 0, 0))
        v_cache_out = lax.dynamic_update_slice(v_cache, as_cache(values), (0, 0, 0, 0))
        halves = w_down.reshape(-1, 2, half)
        down_own = pick(halves, core, 1)
        down_other = pick(halves, 1 - core, 1)
        core_arg = core.astype(jnp.int32).reshape(1)

        outs = []
        for first in range(0, batch_size, CHUNK):
            attn = attend(queries, keys, values, seq_lens, first, CHUNK, seq_len)
            gathered = lax.all_gather(attn, "tp", axis=0)
            hidden, normed = project_out(gathered, w_full, x_rows, mlp_gain, core_arg, first, seq_len)
            normed_other = swap(normed, sibling)
            normed_both = jnp.stack([jnp.where(core == 0, normed, normed_other), jnp.where(core == 0, normed_other, normed)])
            hidden_parts = hidden.reshape(2, block, 2, half)
            give = pick(pick(hidden_parts, bit_first), 1 - core, 1)
            take = swap(give, sibling)
            hidden_mine = jnp.where(bit_first == core, pick(pick(hidden_parts, bit_second), core, 1), take)
            normed_rows = normed_both.reshape(2 * seq_len, width)
            gate_pre = jnp.dot(normed_rows, w_gate, preferred_element_type=F32)
            up_pre = jnp.dot(normed_rows, w_up, preferred_element_type=F32)
            gated = (jax.nn.silu(gate_pre) * up_pre).astype(BF16)
            part_other = jnp.dot(gated, down_other, preferred_element_type=F32).astype(BF16)
            from_sibling = swap(part_other, sibling)
            part_own = lax.reduce_precision(jnp.dot(gated, down_own, preferred_element_type=F32), 8, 7)
            pair = (part_own + from_sibling.astype(F32)).reshape(2, seq_len, half)
            quad = pick(pair, bit_first) + swap(pick(pair, 1 - bit_first), first_axis)
            quad = quad.reshape(2, block, half)
            total = pick(quad, bit_second) + swap(pick(quad, 1 - bit_second), second_axis)
            outs.append((hidden_mine.astype(F32) + total).astype(BF16))

        y = jnp.zeros_like(x)
        for index, rows in enumerate(outs):
            blocks = lax.all_gather(rows, "tp", axis=0).reshape(2, 2, 2, block, half)
            left = jnp.transpose(blocks[:, :, 0], (1, 0, 2, 3))
            piece = jnp.concatenate([left, blocks[:, :, 1]], axis=-1).reshape(CHUNK, seq_len, width)
            y = lax.dynamic_update_slice(y, piece, (index * CHUNK, 0, 0))
        return y, k_cache_out, v_cache_out

    cache_spec = P("dp", None, "tp", None)
    return jax.shard_map(layer_shard, mesh=mesh, in_specs=(P("dp", None, None), P("dp"), P(None, "tp"), P(None, "tp"), P(None, "tp"), P("tp", None), P(None, "tp"), P(None, "tp"), P("tp", None), P(), P(), cache_spec, cache_spec), out_specs=(P("dp", None, None), cache_spec, cache_spec), check_vma=False)
```

time: 2350 us -> 1560 us (0.66)
  blocking collectives: 558 us -> 0 us
  waiting for transfers between devices: 996 us -> 483 us
  Pallas kernels: 0 us -> 304 us
  matrix products: 502 us -> 389 us
  local copies, waits for them, and re-layouts: 137 us -> 212 us
    all_to_all x1 -> x0, blocking collectives: 558 us -> none  [sum_partials(): received = lax.all_to_all(stacked, 'tp', 1, 1, tiled=True)]
    all_to_all x1 -> x0, waiting for transfers between devices: 545 us -> none  [sum_partials(): received = lax.all_to_all(stacked, 'tp', 1, 1, tiled=True)]
    pallas_call x0 -> x9, Pallas kernels: none -> 304 us  [the longest x4 187 us: project_out(): pl.pallas_call(out_kernel, grid_spec=pltpu.PrefetchScalarGridSpec(num_sca...]
    ppermute x0 -> x20, waiting for transfers between devices: none -> 238 us  [solution(): swap = lambda value, pairs: lax.ppermute(value, 'tp', pairs)]
    all_gather x2 -> x9, waiting for transfers between devices: 451 us -> 244 us  [the longest x1 159 us: layer_shard(): w_full = lax.all_gather(w_out, 'tp', axis=0, tiled=True)]
    dot_general x9 -> x16, matrix products: 502 us -> 389 us  [the longest x4 127 us: layer_shard(): up_pre = jnp.dot(normed_rows, w_up, preferred_element_type=F32)]
    reduce_sum x5 -> x0, other arithmetic: 92.4 us -> none  [the longest x2 43.3 us: sum_partials(): summed = jnp.sum(received.astype(jnp.float32), axis=1)]
    transpose x0 -> x8, local copies, waits for them, and re-layouts: none -> 47.5 us  [layer_shard(): left = jnp.transpose(blocks[:, :, 0], (1, 0, 2, 3))]
  transfers between devices with their start and end apart: 3 -> 29, of which waited for: 3 -> 16; matrix products, arithmetic and copies ran while one was open for 0% -> 42% of each run, Pallas kernels for 0% -> 14%
where the time goes in v1:
time: 1560 us; the launch traced here: 1550 us
  waiting for transfers between devices  483 us (31%)
  matrix products  389 us (25%)
  Pallas kernels  304 us (19%)
  local copies, waits for them, and re-layouts  212 us (14%)
  other arithmetic  133 us (9%)
    ppermute x20, waiting for transfers between devices, solution(): swap = lambda value, pairs: lax.ppermute(value, 'tp', pairs)  238 us
    pallas_call x4, Pallas kernels, project_out(): pl.pallas_call(out_kernel, grid_spec=pltpu.PrefetchScalarGridSpec(num_sca...  187 us
    all_gather x1, waiting for transfers between devices, layer_shard(): w_full = lax.all_gather(w_out, 'tp', axis=0, tiled=True)  159 us
    dot_general x4, matrix products, layer_shard(): up_pre = jnp.dot(normed_rows, w_up, preferred_element_type=F32)  127 us
    dot_general x4, matrix products, layer_shard(): gate_pre = jnp.dot(normed_rows, w_gate, preferred_element_type=F32)  124 us
    dot_general x4, matrix products, layer_shard(): jnp.dot(gated, down_own, preferred_element_type=F32)  73.8 us
    pallas_call x1, Pallas kernels, project_qkv(): pl.pallas_call(functools.partial(qkv_kernel, tiles), grid_spec=pltpu.Pref...  66.9 us
    dot_general x4, matrix products, layer_shard(): jnp.dot(gated, down_other, preferred_element_type=F32).astype(BF16)  64.5 us
  transfers between devices with their start and end apart: 29, of which 16 were waited for; matrix products, arithmetic and copies ran while one was open for 42% of the time, Pallas kernels for 14%

profile of v1, /device:TPU:0, one launch (start us, length us, event | category | flops | bytes accessed | tf_op | source)
XLA Modules:
  0.0 1551.0 jit_solution(6983720052930375940)
XLA Ops:
  20.0 66.9 %shard_map.148 = (bf16[6144,512]{1,0:T(8,128)(2,1)}, bf16[6144,128]{1,0:T(8,128)(2,1)}, bf16[6144,128]{1,0:T(8,128)(2,1)}) custom-call(s32[8]{0:T(128)} %lens_ref.9, bf16[6144,4096]{1,0:T(8,128)(2,1)} %bitcast.209, bf16[1,4096]{1,0:T(2,128)(2,1)} %reshape.153.gain_ref, bf16[4096,512]{1,0:T(8,128)(2,1)} %wq_ref.1, ...), custom_call_target="tpu_custom_call" | custom-call | flops 38654705664 | bytes 50331648 | tf_op jit(solution)/shard_map/pallas_call | solution.py:104
  89.7 12.8 shard_map.155
  142.3 18.8 %copy.38 = bf16[1792,4096]{0,1:T(8,128)(2,1)} copy(bf16[1792,4096]{1,0:T(8,128)(2,1)} %param.21) | data formatting | bytes 29360128 | tf_op args[8]
  173.8 158.8 %all-gather.18.cloned.1.call-done.w_ref = bf16[4096,4096]{1,0:T(8,128)(2,1)} async-done(((bf16[512,4096]{1,0:T(8,128)(2,1)}), bf16[4096,4096]{1,0:T(8,128)(2,1)}) %all-gather.18.cloned.1.call-update) | async-done | bytes 33554448 | tf_op jit(solution)/shard_map/all_gather | solution.py:173
  332.6 47.2 %shard_map.156 = (bf16[768,4096]{1,0:T(8,128)(2,1)}, bf16[768,4096]{1,0:T(8,128)(2,1)}) custom-call(s32[1]{0:T(128)} %bitcast.core_ref, bf16[8,1536,512]{2,1,0:T(8,128)(2,1)} %bitcast.271, bf16[4096,4096]{1,0:T(8,128)(2,1)} %all-gather.18.cloned.1.call-done.w_ref, bf16[6144,4096]{1,0:T(8,128)(2,1)} %bitcast.210, bf16[1,4096]{1,0:T(2,128)(2,1)} %reshape.156.gain_ref), custom_call_target="tpu_custom_call" | custom-call | flops 25769803776 | bytes 67108864 | tf_op jit(solution)/shard_map/pallas_call | solution.py:137
  405.2 47.1 %shard_map.154 = (bf16[768,4096]{1,0:T(8,128)(2,1)}, bf16[768,4096]{1,0:T(8,128)(2,1)}) custom-call(s32[1]{0:T(128)} %bitcast.core_ref, bf16[8,1536,512]{2,1,0:T(8,128)(2,1)} %bitcast.270, bf16[4096,4096]{1,0:T(8,128)(2,1)} %all-gather.18.cloned.1.call-done.w_ref, bf16[6144,4096]{1,0:T(8,128)(2,1)} %bitcast.211, bf16[1,4096]{1,0:T(2,128)(2,1)} %reshape.156.gain_ref), custom_call_target="tpu_custom_call" | custom-call | flops 25769803776 | bytes 67108864 | tf_op jit(solution)/shard_map/pallas_call | solution.py:137
  452.8 19.9 %all-gather.24.cloned.1.call-done = bf16[12288,512]{1,0:T(8,128)(2,1)} async-done(((bf16[1536,512]{1,0:T(8,128)(2,1)}), bf16[12288,512]{1,0:T(8,128)(2,1)}) %all-gather.24.cloned.1.call-update) | async-done | bytes 12582928 | tf_op jit(solution)/shard_map/all_gather | solution.py:187
  472.7 47.2 %shard_map.152 = (bf16[768,4096]{1,0:T(8,128)(2,1)}, bf16[768,4096]{1,0:T(8,128)(2,1)}) custom-call(s32[1]{0:T(128)} %bitcast.core_ref, bf16[8,1536,512]{2,1,0:T(8,128)(2,1)} %bitcast.269, bf16[4096,4096]{1,0:T(8,128)(2,1)} %all-gather.18.cloned.1.call-done.w_ref, bf16[6144,4096]{1,0:T(8,128)(2,1)} %bitcast.212, bf16[1,4096]{1,0:T(2,128)(2,1)} %reshape.156.gain_ref), custom_call_target="tpu_custom_call" | custom-call | flops 25769803776 | bytes 67108864 | tf_op jit(solution)/shard_map/pallas_call | solution.py:137
  520.3 22.4 %all-gather.20.cloned.1.call-done = bf16[12288,512]{1,0:T(8,128)(2,1)} async-done(((bf16[1536,512]{1,0:T(8,128)(2,1)}), bf16[12288,512]{1,0:T(8,128)(2,1)}) %all-gather.20.cloned.1.call-update) | async-done | bytes 12582928 | tf_op jit(solution)/shard_map/all_gather | solution.py:187
  542.7 45.3 %shard_map.150 = (bf16[768,4096]{1,0:T(8,128)(2,1)}, bf16[768,4096]{1,0:T(8,128)(2,1)}) custom-call(s32[1]{0:T(128)} %bitcast.core_ref, bf16[8,1536,512]{2,1,0:T(8,128)(2,1)} %bitcast.268, bf16[4096,4096]{1,0:T(8,128)(2,1)} %all-gather.18.cloned.1.call-done.w_ref, bf16[6144,4096]{1,0:T(8,128)(2,1)} %bitcast.213, bf16[1,4096]{1,0:T(2,128)(2,1)} %reshape.156.gain_ref), custom_call_target="tpu_custom_call" | custom-call | flops 25769803776 | bytes 67108864 | tf_op jit(solution)/shard_map/pallas_call | solution.py:137
  598.8 31.8 %fusion.42 = f32[1536,1792]{1,0:T(8,128)} fusion(bf16[1536,4096]{1,0:T(8,128)(2,1)} %bitcast.258, bf16[4096,1792]{1,0:T(8,128)(2,1)} %param.19), kind=kOutput, calls=%fused_computation.116 | convolution fusion | flops 22548578304 | bytes 38273024 | tf_op jit(solution)/shard_map/dot_general | solution.py:196
  630.6 31.9 %multiply_convert_fusion = bf16[1536,1792]{1,0:T(8,128)(2,1)} fusion(f32[1536,1792]{1,0:T(8,128)} %fusion.42, bf16[1536,4096]{1,0:T(8,128)(2,1)} %bitcast.259, bf16[4096,1792]{1,0:T(8,128)(2,1)} %param.20), kind=kOutput, calls=%fused_computation.15 | convolution fusion | flops 22565093376 | bytes 43778048 | tf_op jit(solution)/shard_map/dot_general | solution.py:197
  662.5 15.6 %convolution_convert_fusion = bf16[1536,2048]{1,0:T(8,128)(2,1)} fusion(bf16[1536,1792]{1,0:T(8,128)(2,1)} %multiply_convert_fusion, bf16[1792,2,2048]{0,2,1:T(8,128)(2,1)S(1)} %bitcast.244, s32[]{:T(128)S(6)} %select_n.172), kind=kOutput, calls=%fused_computation.19 | convolution fusion | flops 11277434880 | bytes 19136516 | tf_op jit(solution)/shard_map/dot_general | solution.py:199
  684.9 27.9 %fusion.41 = f32[1536,1792]{1,0:T(8,128)} fusion(bf16[1536,4096]{1,0:T(8,128)(2,1)S(1)} %bitcast.254, bf16[4096,1792]{1,0:T(8,128)(2,1)} %param.19), kind=kOutput, calls=%fused_computation.115 | convolution fusion | flops 22548578304 | bytes 38273024 | tf_op jit(solution)/shard_map/dot_general | solution.py:196
  712.8 19.2 %convert_add_fusion = f32[1536,2048]{1,0:T(8,128)} fusion(bf16[1536,2048]{1,0:T(8,128)(2,1)} %collective-permute-done.17, bf16[1536,1792]{1,0:T(8,128)(2,1)} %multiply_convert_fusion, bf16[1792,2,2048]{0,2,1:T(8,128)(2,1)} %bitcast.236, s32[]{:T(128)S(6)} %select_n.168), kind=kOutput, calls=%fused_computation.11 | convolution fusion | flops 11283726336 | bytes 31719428 | tf_op jit(solution)/shard_map/dot_general | solution.py:201
  739.8 30.4 %multiply_convert_fusion.1 = bf16[1536,1792]{1,0:T(8,128)(2,1)} fusion(f32[1536,1792]{1,0:T(8,128)} %fusion.41, bf16[1536,4096]{1,0:T(8,128)(2,1)S(1)} %bitcast.255, bf16[4096,1792]{1,0:T(8,128)(2,1)} %param.20), kind=kOutput, calls=%fused_computation.16 | convolution fusion | flops 22565093376 | bytes 43778048 | tf_op jit(solution)/shard_map/dot_general | solution.py:197
  770.1 39.5 %collective-permute-done.18 = f32[768,2048]{1,0:T(8,128)} collective-permute-done((f32[768,2048]{1,0:T(8,128)}, f32[768,2048]{1,0:T(8,128)}, u32[]{:S(2)}, u32[]{:S(2)}) %collective-permute-start.18) | collective-permute-done | bytes 6291488 | tf_op jit(solution)/shard_map/ppermute | solution.py:158
  816.9 17.8 %convolution_convert_fusion.1 = bf16[1536,2048]{1,0:T(8,128)(2,1)} fusion(bf16[1536,1792]{1,0:T(8,128)(2,1)} %multiply_convert_fusion.1, bf16[1792,2,2048]{0,2,1:T(8,128)(2,1)} %bitcast.237, s32[]{:T(128)S(6)} %select_n.172), kind=kOutput, calls=%fused_computation.20 | convolution fusion | flops 11277434880 | bytes 19136516 | tf_op jit(solution)/shard_map/dot_general | solution.py:199
  858.7 32.8 %fusion.40 = f32[1536,1792]{1,0:T(8,128)} fusion(bf16[1536,4096]{1,0:T(8,128)(2,1)} %bitcast.252, bf16[4096,1792]{1,0:T(8,128)(2,1)} %param.19), kind=kOutput, calls=%fused_computation.114 | convolution fusion | flops 22548578304 | bytes 38273024 | tf_op jit(solution)/shard_map/dot_general | solution.py:196
  891.5 17.2 %convert_add_fusion.1 = f32[1536,2048]{1,0:T(8,128)S(1)} fusion(bf16[1536,2048]{1,0:T(8,128)(2,1)} %collective-permute-done.12, bf16[1536,1792]{1,0:T(8,128)(2,1)} %multiply_convert_fusion.1, bf16[1792,2,2048]{0,2,1:T(8,128)(2,1)} %bitcast.238, s32[]{:T(128)S(6)} %select_n.168), kind=kOutput, calls=%fused_computation.12 | convolution fusion | flops 11283726336 | bytes 31719428 | tf_op jit(solution)/shard_map/dot_general | solution.py:201
  918.7 32.9 %multiply_convert_fusion.2 = bf16[1536,1792]{1,0:T(8,128)(2,1)} fusion(f32[1536,1792]{1,0:T(8,128)} %fusion.40, bf16[1536,4096]{1,0:T(8,128)(2,1)} %bitcast.253, bf16[4096,1792]{1,0:T(8,128)(2,1)} %param.20), kind=kOutput, calls=%fused_computation.17 | convolution fusion | flops 22565093376 | bytes 43778048 | tf_op jit(solution)/shard_map/dot_general | solution.py:197
  951.6 15.2 convolution_convert_fusion.2
  966.9 25.9 %collective-permute-done.13 = f32[768,2048]{1,0:T(8,128)} collective-permute-done((f32[768,2048]{1,0:T(8,128)}, f32[768,2048]{1,0:T(8,128)}, u32[]{:S(2)}, u32[]{:S(2)}) %collective-permute-start.13) | collective-permute-done | bytes 6291488 | tf_op jit(solution)/shard_map/ppermute | solution.py:158
  1077.1 20.5 %convert_add_fusion.2 = f32[1536,2048]{1,0:T(8,128)} fusion(bf16[1536,2048]{1,0:T(8,128)(2,1)} %collective-permute-done.7, bf16[1536,1792]{1,0:T(8,128)(2,1)} %multiply_convert_fusion.2, bf16[1792,2,2048]{0,2,1:T(8,128)(2,1)} %bitcast.239, s32[]{:T(128)S(6)} %select_n.168), kind=kOutput, calls=%fused_computation.13 | convolution fusion | flops 11283726336 | bytes 31719428 | tf_op jit(solution)/shard_map/dot_general | solution.py:201
  1110.7 31.6 %fusion.39 = f32[1536,1792]{1,0:T(8,128)} fusion(bf16[1536,4096]{1,0:T(8,128)(2,1)} %bitcast.256, bf16[4096,1792]{1,0:T(8,128)(2,1)} %param.19), kind=kOutput, calls=%fused_computation.113 | convolution fusion | flops 22548578304 | bytes 38273024 | tf_op jit(solution)/shard_map/dot_general | solution.py:196
  1142.4 38.4 %collective-permute-done.8 = f32[768,2048]{1,0:T(8,128)} collective-permute-done((f32[768,2048]{1,0:T(8,128)}, f32[768,2048]{1,0:T(8,128)}, u32[]{:S(2)}, u32[]{:S(2)}) %collective-permute-start.8) | collective-permute-done | bytes 6291488 | tf_op jit(solution)/shard_map/ppermute | solution.py:158
  1188.5 31.7 %multiply_convert_fusion.3 = bf16[1536,1792]{1,0:T(8,128)(2,1)} fusion(f32[1536,1792]{1,0:T(8,128)} %fusion.39, bf16[1536,4096]{1,0:T(8,128)(2,1)} %bitcast.257, bf16[4096,1792]{1,0:T(8,128)(2,1)} %param.20), kind=kOutput, calls=%fused_computation.18 | convolution fusion | flops 22565093376 | bytes 43778048 | tf_op jit(solution)/shard_map/dot_general | solution.py:197
  1227.5 15.9 %convolution_convert_fusion.3 = bf16[1536,2048]{1,0:T(8,128)(2,1)S(1)} fusion(bf16[1536,1792]{1,0:T(8,128)(2,1)} %multiply_convert_fusion.3, bf16[1792,2,2048]{0,2,1:T(8,128)(2,1)} %bitcast.240, s32[]{:T(128)S(6)} %select_n.172), kind=kOutput, calls=%fused_computation.22 | convolution fusion | flops 11277434880 | bytes 19136516 | tf_op jit(solution)/shard_map/dot_general | solution.py:199
  1253.9 16.8 %convert_add_fusion.3 = f32[1536,2048]{1,0:T(8,128)S(1)} fusion(bf16[1536,2048]{1,0:T(8,128)(2,1)} %collective-permute-done.2, bf16[1536,1792]{1,0:T(8,128)(2,1)} %multiply_convert_fusion.3, bf16[1792,2,2048]{0,2,1:T(8,128)(2,1)} %bitcast.241, s32[]{:T(128)S(6)} %select_n.168), kind=kOutput, calls=%fused_computation.14 | convolution fusion | flops 11283726336 | bytes 31719428 | tf_op jit(solution)/shard_map/dot_general | solution.py:201
  1277.1 85.4 %collective-permute-done.3 = f32[768,2048]{1,0:T(8,128)} collective-permute-done((f32[768,2048]{1,0:T(8,128)S(1)}, f32[768,2048]{1,0:T(8,128)}, u32[]{:S(2)}, u32[]{:S(2)}) %collective-permute-start.3) | collective-permute-done | bytes 6291488 | tf_op jit(solution)/shard_map/ppermute | solution.py:158
  1454.8 30.3 %all-gather.22.cloned.1.call-done = bf16[3072,2048]{1,0:T(8,128)(2,1)} async-done(((bf16[384,2048]{1,0:T(8,128)(2,1)}), bf16[3072,2048]{1,0:T(8,128)(2,1)}) %all-gather.22.cloned.1.call-update) | async-done | bytes 12582928 | tf_op jit(solution)/shard_map/all_gather | solution.py:210
  1497.0 20.3 %fusion.2 = bf16[8,768,4096]{2,1,0:T(8,128)(2,1)} fusion(bf16[2,768,2048]{2,1,0:T(8,128)(2,1)} %bitcast.235, bf16[2,768,2048]{2,1,0:T(8,128)(2,1)} %bitcast.234), kind=kLoop, calls=%fused_computation.3 | loop fusion | flops 176160768 | bytes 62914560 | tf_op jit(solution)/shard_map/concatenate | solution.py:212
  (196 shorter events, 420.5 us)
Async XLA Ops:
  7.2 166.6 %all-gather.32.cloned.1.call-start = ((), (), s32[]{:S(2)}) async-start(), calls=%async_computation.7 | async-start | bytes 14155776 | tf_op jit(solution)/shard_map/all_gather | solution.py:187
  20.0 66.9 %copy-start.4 = (s32[8]{0:T(128)S(1)}, s32[8]{0:T(128)}, u32[]{:S(2)}) copy-start(s32[8]{0:T(128)} %lens_ref.9) | copy-start | bytes 100
  102.6 230.0 %all-gather.18.cloned.1.call-start = ((), (), s32[]{:S(2)}) async-start(), calls=%async_computation | async-start | bytes 37748736 | tf_op jit(solution)/shard_map/all_gather | solution.py:173
  103.3 301.9 %all-gather.28.cloned.1.call-start = ((), (), s32[]{:S(2)}) async-start(), calls=%async_computation.5 | async-start | bytes 14155776 | tf_op jit(solution)/shard_map/all_gather | solution.py:187
  116.3 356.4 %all-gather.24.cloned.1.call-start = ((), (), s32[]{:S(2)}) async-start(), calls=%async_computation.3 | async-start | bytes 14155776 | tf_op jit(solution)/shard_map/all_gather | solution.py:187
  128.9 413.7 %all-gather.20.cloned.1.call-start = ((), (), s32[]{:S(2)}) async-start(), calls=%async_computation.1 | async-start | bytes 14155776 | tf_op jit(solution)/shard_map/all_gather | solution.py:187
  141.6 1277.5 %all-gather.34.cloned.1.call-start = ((), (), s32[]{:S(2)}) async-start(), calls=%async_computation.8 | async-start | bytes 14155776 | tf_op jit(solution)/shard_map/all_gather | solution.py:210
  379.8 208.4 %collective-permute-start.16 = (bf16[768,4096]{1,0:T(8,128)(2,1)}, bf16[768,4096]{1,0:T(8,128)(2,1)}, u32[]{:S(2)}, u32[]{:S(2)}) collective-permute-start(bf16[768,4096]{1,0:T(8,128)(2,1)} %get-tuple-element.24), channel_id=1, source_target_pairs={{0,1},{1,0},{2,3},{3,2},{4,5},{5,4},{6,7},{7,6},{8,9},{9,8},{10,11... | collective-permute-start | bytes 18874376 | tf_op jit(solution)/shard_map/ppermute | solution.py:158
  405.0 439.2 %collective-permute-start.15 = (bf16[384,2048]{1,0:T(8,128)(2,1)}, bf16[384,2048]{1,0:T(8,128)(2,1)}, u32[]{:S(2)}, u32[]{:S(2)}) collective-permute-start(bf16[384,2048]{1,0:T(8,128)(2,1)} %bitcast.203), channel_id=1, source_target_pairs={{0,1},{1,0},{2,3},{3,2},{4,5},{5,4},{6,7},{7,6},{8,9},{9,8},{10,11... | collective-permute-start | bytes 4718600 | tf_op jit(solution)/shard_map/ppermute | solution.py:158
  452.3 226.0 %collective-permute-start.11 = (bf16[768,4096]{1,0:T(8,128)(2,1)}, bf16[768,4096]{1,0:T(8,128)(2,1)}, u32[]{:S(2)}, u32[]{:S(2)}) collective-permute-start(bf16[768,4096]{1,0:T(8,128)(2,1)} %get-tuple-element.22), channel_id=1, source_target_pairs={{0,1},{1,0},{2,3},{3,2},{4,5},{5,4},{6,7},{7,6},{8,9},{9,8},{10,11... | collective-permute-start | bytes 18874376 | tf_op jit(solution)/shard_map/ppermute | solution.py:158
  519.8 314.8 %collective-permute-start.6 = (bf16[768,4096]{1,0:T(8,128)(2,1)}, bf16[768,4096]{1,0:T(8,128)(2,1)}, u32[]{:S(2)}, u32[]{:S(2)}) collective-permute-start(bf16[768,4096]{1,0:T(8,128)(2,1)} %get-tuple-element.20), channel_id=1, source_target_pairs={{0,1},{1,0},{2,3},{3,2},{4,5},{5,4},{6,7},{7,6},{8,9},{9,8},{10,11... | collective-permute-start | bytes 18874376 | tf_op jit(solution)/shard_map/ppermute | solution.py:158
  587.9 484.0 %collective-permute-start.1 = (bf16[768,4096]{1,0:T(8,128)(2,1)}, bf16[768,4096]{1,0:T(8,128)(2,1)}, u32[]{:S(2)}, u32[]{:S(2)}) collective-permute-start(bf16[768,4096]{1,0:T(8,128)(2,1)} %get-tuple-element.18), channel_id=1, source_target_pairs={{0,1},{1,0},{2,3},{3,2},{4,5},{5,4},{6,7},{7,6},{8,9},{9,8},{10,11... | collective-permute-start | bytes 18874376 | tf_op jit(solution)/shard_map/ppermute | solution.py:158
  598.8 63.7 %slice-start.6 = ((s8[14680064]{0:T(1024)(128)(4,1)}), s8[4194304]{0:T(1024)(128)(4,1)S(1)}, s32[]{:S(2)}) async-start(s8[14680064]{0:T(1024)(128)(4,1)} %bitcast.242), calls=%async_computation.15 | async-start | bytes 8388608
  598.8 63.7 %slice-start.7 = ((s8[14680064]{0:T(1024)(128)(4,1)}), s8[4194304]{0:T(1024)(128)(4,1)S(1)}, s32[]{:S(2)}) async-start(s8[14680064]{0:T(1024)(128)(4,1)} %bitcast.242), calls=%async_computation.16 | async-start | bytes 8388608
  678.2 34.6 %collective-permute-start.17 = (bf16[1536,2048]{1,0:T(8,128)(2,1)}, bf16[1536,2048]{1,0:T(8,128)(2,1)}, u32[]{:S(2)}, u32[]{:S(2)}) collective-permute-start(bf16[1536,2048]{1,0:T(8,128)(2,1)} %convolution_convert_fusion), channel_id=1, source_target_pairs={{0,1},{1,0},{2,3},{3,2},{4,5},{5,4},{6,7},{7,6},{8,9},{9,8},{10,11... | collective-permute-start | bytes 18874376 | tf_op jit(solution)/shard_map/ppermute | solution.py:158
  738.3 71.3 %collective-permute-start.18 = (f32[768,2048]{1,0:T(8,128)}, f32[768,2048]{1,0:T(8,128)}, u32[]{:S(2)}, u32[]{:S(2)}) collective-permute-start(f32[768,2048]{1,0:T(8,128)} %dynamic-slice_bitcast_fusion), channel_id=1, source_target_pairs={{0,2},{1,5},{2,0},{3,7},{4,6},{5,1},{6,4},{7,3},{8,10},{9,13},{10,... | collective-permute-start | bytes 18874376 | tf_op jit(solution)/shard_map/ppermute | solution.py:158
  815.9 37.4 %collective-permute-start.19 = (f32[384,2048]{1,0:T(8,128)S(1)}, f32[384,2048]{1,0:T(8,128)}, u32[]{:S(2)}, u32[]{:S(2)}) collective-permute-start(f32[384,2048]{1,0:T(8,128)S(1)} %dynamic-slice_bitcast_fusion.4), channel_id=1, source_target_pairs={{0,4},{1,3},{2,6},{3,1},{4,0},{5,7},{6,2},{7,5},{8,12},{9,11},{10,... | collective-permute-start | bytes 9437192 | tf_op jit(solution)/shard_map/ppermute | solution.py:158
  834.7 56.9 %collective-permute-start.12 = (bf16[1536,2048]{1,0:T(8,128)(2,1)}, bf16[1536,2048]{1,0:T(8,128)(2,1)}, u32[]{:S(2)}, u32[]{:S(2)}) collective-permute-start(bf16[1536,2048]{1,0:T(8,128)(2,1)} %convolution_convert_fusion.1), channel_id=1, source_target_pairs={{0,1},{1,0},{2,3},{3,2},{4,5},{5,4},{6,7},{7,6},{8,9},{9,8},{10,11... | collective-permute-start | bytes 18874376 | tf_op jit(solution)/shard_map/ppermute | solution.py:158
  858.7 572.2 %all-gather.30.cloned.1.call-start = ((), (), s32[]{:S(2)}) async-start(), calls=%async_computation.6 | async-start | bytes 14155776 | tf_op jit(solution)/shard_map/all_gather | solution.py:210
  916.8 76.0 %collective-permute-start.13 = (f32[768,2048]{1,0:T(8,128)}, f32[768,2048]{1,0:T(8,128)}, u32[]{:S(2)}, u32[]{:S(2)}) collective-permute-start(f32[768,2048]{1,0:T(8,128)} %dynamic-slice_bitcast_fusion.1), channel_id=1, source_target_pairs={{0,2},{1,5},{2,0},{3,7},{4,6},{5,1},{6,4},{7,3},{8,10},{9,13},{10,... | collective-permute-start | bytes 18874376 | tf_op jit(solution)/shard_map/ppermute | solution.py:158
  966.9 110.3 %collective-permute-start.7 = (bf16[1536,2048]{1,0:T(8,128)(2,1)}, bf16[1536,2048]{1,0:T(8,128)(2,1)}, u32[]{:S(2)}, u32[]{:S(2)}) collective-permute-start(bf16[1536,2048]{1,0:T(8,128)(2,1)} %convolution_convert_fusion.2), channel_id=1, source_target_pairs={{0,1},{1,0},{2,3},{3,2},{4,5},{5,4},{6,7},{7,6},{8,9},{9,8},{10,11... | collective-permute-start | bytes 18874376 | tf_op jit(solution)/shard_map/ppermute | solution.py:158
  1003.2 37.6 %collective-permute-start.14 = (f32[384,2048]{1,0:T(8,128)}, f32[384,2048]{1,0:T(8,128)}, u32[]{:S(2)}, u32[]{:S(2)}) collective-permute-start(f32[384,2048]{1,0:T(8,128)} %dynamic-slice_bitcast_fusion.5), channel_id=1, source_target_pairs={{0,4},{1,3},{2,6},{3,1},{4,0},{5,7},{6,2},{7,5},{8,12},{9,11},{10,... | collective-permute-start | bytes 9437192 | tf_op jit(solution)/shard_map/ppermute | solution.py:158
  1027.9 3.4 collective-permute-start.10
  1047.1 395.5 %all-gather.26.cloned.1.call-start = ((), (), s32[]{:S(2)}) async-start(), calls=%async_computation.4 | async-start | bytes 14155776 | tf_op jit(solution)/shard_map/all_gather | solution.py:210
  1071.9 148.3 %collective-permute-start.5 = (bf16[384,2048]{1,0:T(8,128)(2,1)}, bf16[384,2048]{1,0:T(8,128)(2,1)}, u32[]{:S(2)}, u32[]{:S(2)}) collective-permute-start(bf16[384,2048]{1,0:T(8,128)(2,1)} %bitcast.205), channel_id=1, source_target_pairs={{0,1},{1,0},{2,3},{3,2},{4,5},{5,4},{6,7},{7,6},{8,9},{9,8},{10,11... | collective-permute-start | bytes 4718600 | tf_op jit(solution)/shard_map/ppermute | solution.py:158
  1104.0 76.7 %collective-permute-start.8 = (f32[768,2048]{1,0:T(8,128)}, f32[768,2048]{1,0:T(8,128)}, u32[]{:S(2)}, u32[]{:S(2)}) collective-permute-start(f32[768,2048]{1,0:T(8,128)} %dynamic-slice_bitcast_fusion.2), channel_id=1, source_target_pairs={{0,2},{1,5},{2,0},{3,7},{4,6},{5,1},{6,4},{7,3},{8,10},{9,13},{10,... | collective-permute-start | bytes 18874376 | tf_op jit(solution)/shard_map/ppermute | solution.py:158
  1187.0 37.3 %collective-permute-start.9 = (f32[384,2048]{1,0:T(8,128)S(1)}, f32[384,2048]{1,0:T(8,128)S(1)}, u32[]{:S(2)}, u32[]{:S(2)}) collective-permute-start(f32[384,2048]{1,0:T(8,128)S(1)} %dynamic-slice_bitcast_fusion.6), channel_id=1, source_target_pairs={{0,4},{1,3},{2,6},{3,1},{4,0},{5,7},{6,2},{7,5},{8,12},{9,11},{10,... | collective-permute-start | bytes 9437192 | tf_op jit(solution)/shard_map/ppermute | solution.py:158
  1227.4 257.7 %all-gather.22.cloned.1.call-start = ((), (), s32[]{:S(2)}) async-start(), calls=%async_computation.2 | async-start | bytes 14155776 | tf_op jit(solution)/shard_map/all_gather | solution.py:210
  1243.3 10.6 collective-permute-start.2
  1275.6 86.9 %collective-permute-start.3 = (f32[768,2048]{1,0:T(8,128)S(1)}, f32[768,2048]{1,0:T(8,128)}, u32[]{:S(2)}, u32[]{:S(2)}) collective-permute-start(f32[768,2048]{1,0:T(8,128)S(1)} %dynamic-slice_bitcast_fusion.3), channel_id=1, source_target_pairs={{0,2},{1,5},{2,0},{3,7},{4,6},{5,1},{6,4},{7,3},{8,10},{9,13},{10,... | collective-permute-start | bytes 18874376 | tf_op jit(solution)/shard_map/ppermute | solution.py:158
  1372.9 37.6 %collective-permute-start.4 = (f32[384,2048]{1,0:T(8,128)}, f32[384,2048]{1,0:T(8,128)}, u32[]{:S(2)}, u32[]{:S(2)}) collective-permute-start(f32[384,2048]{1,0:T(8,128)} %dynamic-slice_bitcast_fusion.7), channel_id=1, source_target_pairs={{0,4},{1,3},{2,6},{3,1},{4,0},{5,7},{6,2},{7,5},{8,12},{9,11},{10,... | collective-permute-start | bytes 9437192 | tf_op jit(solution)/shard_map/ppermute | solution.py:158
  1397.8 3.4 collective-permute-start
  (29 other events, 519.7 us)
Sparse Core Ops, SparseCore 0:
  102.7 71.0 all-gather.31
  175.6 156.9 all-gather.17
  334.4 68.2 all-gather.27
  404.4 68.2 all-gather.23
  474.4 68.2 all-gather.19
  858.8 72.0 all-gather.33
  1047.2 71.3 all-gather.29
  1227.5 77.9 all-gather.25
  1416.8 68.2 all-gather.21

commit v2 on v1

v2 whole, which is shorter than its diff:
```python
import functools

import jax
import jax.numpy as jnp
from jax import lax
from jax.experimental import pallas as pl
from jax.experimental.pallas import tpu as pltpu
from jax.sharding import PartitionSpec as P


EPS = 1e-5
ROPE_BASE = 10000.0
F32 = jnp.float32
BF16 = jnp.bfloat16
PIECES = (1,2,2,2,1)
TILE = 256


def rms_rows(rows, gain):
    rows32 = rows.astype(F32)
    inv_rms = lax.rsqrt(jnp.mean(rows32 * rows32, axis=-1, keepdims=True) + EPS)
    return (rows32 * inv_rms * gain.astype(F32)).astype(BF16)


def qkv_kernel(tiles, lens_ref, x_ref, gain_ref, wq_ref, wkv_ref, cos_ref, sin_ref, q_ref, k_ref, v_ref):
    step = pl.program_id(0)
    normed = rms_rows(x_ref[...], gain_ref[...])
    head = cos_ref.shape[1]
    cos_tab = cos_ref[...]
    sin_tab = sin_ref[...]
    even = lax.broadcasted_iota(jnp.int32, cos_tab.shape, 1) % 2 == 0

    def turn(part):
        swapped = jnp.where(even, pltpu.roll(part, head - 1, 1), pltpu.roll(part, 1, 1))
        return (part * cos_tab + swapped * sin_tab).astype(BF16)

    kv = jnp.dot(normed, wkv_ref[...], preferred_element_type=F32)
    rows = lax.rem(step, tiles) * cos_tab.shape[0] + lax.broadcasted_iota(jnp.int32, cos_tab.shape, 0)
    valid = rows < lens_ref[step // tiles]
    zero = jnp.zeros(cos_tab.shape, BF16)
    k_ref[...] = jnp.where(valid, turn(kv[:, :head]), zero)
    v_ref[...] = jnp.where(valid, kv[:, head:].astype(BF16), zero)
    queries = jnp.dot(normed, wq_ref[...], preferred_element_type=F32)
    for h in range(queries.shape[1] // head):
        cols = slice(h * head, (h + 1) * head)
        q_ref[:, cols] = turn(queries[:, cols])


def attention_kernel(lens_ref, seq_ref, q_ref, k_ref, v_ref, *o_refs):
    step = pl.program_id(0)
    length = lens_ref[seq_ref[step]]
    seq_len, head = k_ref.shape
    scale = head ** -0.5

    def run(o_ref):
        for tile in range(seq_len // TILE):
            width = (tile + 1) * TILE
            rows = slice(tile * TILE, (tile + 1) * TILE)
            query_at = tile * TILE + lax.broadcasted_iota(jnp.int32, (TILE, width), 0)
            key_at = lax.broadcasted_iota(jnp.int32, (TILE, width), 1)
            allowed = (key_at <= query_at) & (key_at < length)
            for h in range(q_ref.shape[1] // head):
                cols = slice(h * head, (h + 1) * head)
                scores = lax.dot_general(q_ref[rows, cols], k_ref[:width, :], (((1,), (1,)), ((), ())), preferred_element_type=F32)
                scores = jnp.where(allowed, scores * scale, -jnp.inf)
                top = jnp.max(scores, axis=-1, keepdims=True)
                weights = jnp.exp(scores - top)
                probs = (weights / jnp.sum(weights, axis=-1, keepdims=True)).astype(BF16)
                o_ref[rows, cols] = jnp.dot(probs, v_ref[:width, :], preferred_element_type=F32).astype(BF16)

    for which, o_ref in enumerate(o_refs):
        @pl.when(step == which)
        def _():
            run(o_ref)


def out_kernel(place_ref, *refs):
    pairs, (w_ref, x_ref, gain_ref, h_ref, n_ref, total) = refs[:-6], refs[-6:]
    step = pl.program_id(0)
    core = place_ref[0]
    depth = w_ref.shape[0] // 2
    tile = x_ref.shape[0]
    at_rows = pl.ds(pl.multiple_of(pl.program_id(1) * tile, tile), tile)
    cols = 1024

    for which, o_ref in enumerate(pairs):
        @pl.when(step == which)
        def _():
            for col in range(0, total.shape[1], cols):
                at = slice(col, col + cols)
                own = jnp.dot(o_ref[:, :depth], w_ref[pl.ds(pl.multiple_of(core * depth, depth), depth), at], preferred_element_type=F32).astype(BF16)
                other = jnp.dot(o_ref[:, depth:], w_ref[pl.ds(pl.multiple_of((1 - core) * depth, depth), depth), at], preferred_element_type=F32).astype(BF16)
                both = own.astype(F32) + other.astype(F32)
                total[at_rows, at] = both if which == 0 else total[at_rows, at] + both

    @pl.when(step == pl.num_programs(0) - 1)
    def _():
        hidden = (x_ref[...].astype(F32) + total[at_rows, :]).astype(BF16)
        h_ref[...] = hidden
        n_ref[...] = rms_rows(hidden, gain_ref[...])


def rope_tables(seq_len, head):
    inv_freq = ROPE_BASE ** (-jnp.arange(0, head, 2).astype(F32) / head)
    angles = jnp.arange(seq_len).astype(F32)[:, None] * inv_freq[None, :]
    sign = jnp.where(jnp.arange(head) % 2 == 0, -1.0, 1.0).astype(F32)
    return jnp.repeat(jnp.cos(angles), 2, axis=1), jnp.repeat(jnp.sin(angles), 2, axis=1) * sign


def vmem_limit(mib):
    return dict(vmem_limit_bytes=mib * 2 ** 20)


def project_qkv(x_rows, gain, w_query, w_kv, seq_lens, seq_len, head):
    rows, width = x_rows.shape
    tiles = seq_len // TILE
    cos_tab, sin_tab = rope_tables(seq_len, head)
    whole = lambda shape: pl.BlockSpec(shape, lambda i, s: (0, 0))
    table = pl.BlockSpec((TILE, head), lambda i, s: (lax.rem(i, tiles), 0))
    by_row = lambda cols: pl.BlockSpec((TILE, cols), lambda i, s: (i, 0))
    q_cols = w_query.shape[1]
    return pl.pallas_call(
        functools.partial(qkv_kernel, tiles),
        grid_spec=pltpu.PrefetchScalarGridSpec(
            num_scalar_prefetch=1, grid=(rows // TILE,),
            in_specs=[by_row(width), whole((1, width)), whole(w_query.shape), whole(w_kv.shape), table, table],
            out_specs=[by_row(q_cols), by_row(head), by_row(head)]),
        out_shape=[jax.ShapeDtypeStruct((rows, q_cols), BF16)] + [jax.ShapeDtypeStruct((rows, head), BF16)] * 2,
        compiler_params=pltpu.CompilerParams(**vmem_limit(56)),
        cost_estimate=pl.CostEstimate(flops=2 * rows * width * (q_cols + 2 * head), bytes_accessed=2 * rows * width, transcendentals=0),
    )(seq_lens, x_rows, gain.reshape(1, -1), w_query, w_kv, cos_tab, sin_tab)


def attend(queries, keys, values, seq_lens, order, seq_len):
    q_cols, head = queries.shape[1], keys.shape[1]
    count = order.shape[0]
    by_seq = lambda cols: pl.BlockSpec((seq_len, cols), lambda i, s, o: (o[i], 0))
    return pl.pallas_call(
        attention_kernel,
        grid_spec=pltpu.PrefetchScalarGridSpec(
            num_scalar_prefetch=2, grid=(count,),
            in_specs=[by_seq(q_cols), by_seq(head), by_seq(head)],
            out_specs=[pl.BlockSpec((seq_len, q_cols), lambda i, s, o: (0, 0))] * count),
        out_shape=[jax.ShapeDtypeStruct((seq_len, q_cols), BF16)] * count,
        compiler_params=pltpu.CompilerParams(**vmem_limit(48)),
        cost_estimate=pl.CostEstimate(flops=count * 6 * 10 ** 9, bytes_accessed=count * 2 * 10 ** 6, transcendentals=0),
    )(seq_lens, order, queries, keys, values)


def project_out(pairs, w_full, x_rows, gain, places, first):
    rows, pair_cols = pairs[0].shape
    width = w_full.shape[1]
    tile = 384
    last = len(pairs) - 1
    row_block = pl.BlockSpec((tile, width), lambda i, r, c: (jnp.where(i == last, r, 0), 0))
    return pl.pallas_call(
        out_kernel,
        grid_spec=pltpu.PrefetchScalarGridSpec(
            num_scalar_prefetch=1, grid=(len(pairs), rows // tile),
            in_specs=[pl.BlockSpec((tile, pair_cols), lambda i, r, c, j=j: (jnp.where(i == j, r, 0 if rows == tile else jnp.where(i < j, 0, rows // tile - 1)), 0)) for j in range(len(pairs))]
                     + [pl.BlockSpec((pair_cols, width), lambda i, r, c: (c[1 + i], 0)),
                        pl.BlockSpec((tile, width), lambda i, r, c: ((first + c[0] * rows) // tile + jnp.where(i == last, r, 0), 0)),
                        pl.BlockSpec((1, width), lambda i, r, c: (0, 0))],
            out_specs=[row_block, row_block],
            scratch_shapes=[pltpu.VMEM((rows, width), F32)]),
        out_shape=[jax.ShapeDtypeStruct((rows, width), BF16)] * 2,
        compiler_params=pltpu.CompilerParams(**vmem_limit(62)),
        cost_estimate=pl.CostEstimate(flops=2 * rows * width * len(pairs) * pair_cols, bytes_accessed=4 * width * width, transcendentals=0),
    )(places, *pairs, w_full, x_rows, gain.reshape(1, -1))


def gate_kernel(tiles, mine_ref, other_ref, gate_ref, up_ref, gated_ref):
    step = pl.program_id(0)

    def run(rows_ref):
        gate_pre = jnp.dot(rows_ref[...], gate_ref[...], preferred_element_type=F32)
        up_pre = jnp.dot(rows_ref[...], up_ref[...], preferred_element_type=F32)
        gated_ref[...] = (jax.nn.silu(gate_pre) * up_pre).astype(BF16)

    @pl.when(step < tiles)
    def _():
        run(mine_ref)

    @pl.when(step >= tiles)
    def _():
        run(other_ref)


def gate_up(mine, other, w_gate, w_up):
    rows, width = mine.shape
    hidden = w_gate.shape[1]
    tile = min(rows, 768)
    tiles = rows // tile
    weights = pl.BlockSpec((width, TILE), lambda r, f: (0, f))
    return pl.pallas_call(
        functools.partial(gate_kernel, tiles),
        grid=(2 * tiles, hidden // TILE),
        in_specs=[pl.BlockSpec((tile, width), lambda r, f: (jnp.minimum(r, tiles - 1), 0)),
                  pl.BlockSpec((tile, width), lambda r, f: (jnp.maximum(r - tiles, 0), 0)), weights, weights],
        out_specs=pl.BlockSpec((tile, TILE), lambda r, f: (r, f)),
        out_shape=jax.ShapeDtypeStruct((2 * rows, hidden), BF16),
        compiler_params=pltpu.CompilerParams(**vmem_limit(60)),
        cost_estimate=pl.CostEstimate(flops=8 * rows * width * hidden, bytes_accessed=8 * rows * width, transcendentals=0),
    )(mine, other, w_gate, w_up)


def place_kernel(blocks_ref, *refs):
    refs[-1][...] = blocks_ref[0]


def place_rows(y_rows, blocks, first):
    count, rows, cols = blocks.shape

    def where(k):
        at_y, at_x, core = k // 4, lax.rem(k // 2, 2), lax.rem(k, 2)
        along = jnp.where(core == 0, 2 * at_x + at_y, 2 * at_y + at_x)
        return first + along, core

    fresh = isinstance(y_rows, jax.ShapeDtypeStruct)
    return pl.pallas_call(
        place_kernel,
        grid=(count,),
        in_specs=[pl.BlockSpec((1, rows, cols), lambda k: (k, 0, 0))] + ([] if fresh else [pl.BlockSpec(memory_space=pl.ANY)]),
        out_specs=pl.BlockSpec((rows, cols), where),
        out_shape=jax.ShapeDtypeStruct(y_rows.shape, y_rows.dtype),
        input_output_aliases={} if fresh else {1: 0},
        compiler_params=pltpu.CompilerParams(**vmem_limit(60)),
        cost_estimate=pl.CostEstimate(flops=4 * 10 ** 9, bytes_accessed=2 * blocks.size * 2, transcendentals=0),
    )(blocks, *([] if fresh else [y_rows]))


def after(value, *tokens):
    return lax.optimization_barrier((value,) + tokens)[0]


def solution(mesh):
    tp_size = mesh.shape["tp"]
    sibling = [(i, i ^ 1) for i in range(tp_size)]
    first_axis = [(i, i ^ (4 if i % 2 else 2)) for i in range(tp_size)]
    second_axis = [(i, i ^ (2 if i % 2 else 4)) for i in range(tp_size)]

    def swap(value, pairs):
        return lax.ppermute(value, "tp", pairs)

    def layer_shard(x, seq_lens, w_query, w_key, w_value, w_out, w_gate, w_up, w_down, attn_gain, mlp_gain, k_cache, v_cache):
        batch_size, seq_len, width = x.shape
        head = k_cache.shape[3]
        half = width // 2
        me = lax.axis_index("tp")
        core = me % 2
        at_x = (me // 2) % 2
        at_y = me // 4
        bit_first = jnp.where(core == 0, at_x, at_y)
        bit_second = jnp.where(core == 0, at_y, at_x)
        rows_of = lambda value, index, count: lax.dynamic_slice_in_dim(value, index * count, count, 0)

        w_full = lax.all_gather(w_out, "tp", axis=0, tiled=True)
        x_rows = x.reshape(batch_size * seq_len, width)
        queries, keys, values = project_qkv(x_rows, attn_gain, w_query, jnp.concatenate([w_key, w_value], axis=1), seq_lens, seq_len, head)
        as_cache = lambda rows: rows.reshape(batch_size, seq_len, 1, head)
        k_cache_out = lax.dynamic_update_slice(k_cache, as_cache(keys), (0, 0, 0, 0))
        v_cache_out = lax.dynamic_update_slice(v_cache, as_cache(values), (0, 0, 0, 0))
        down_own = lax.dynamic_slice_in_dim(w_down, core * half, half, 1)
        down_other = lax.dynamic_slice_in_dim(w_down, (1 - core) * half, half, 1)
        chip = me // 2
        along_first = jnp.where(core == 0, 1, 2)
        places = jnp.stack([core, chip, chip ^ along_first, chip ^ (3 - along_first), chip ^ 3]).astype(jnp.int32)

        starts = [sum(PIECES[:p]) for p in range(len(PIECES))]
        count = len(PIECES)
        arrived = []
        lens = seq_lens
        for p in range(count):
            if PIECES[p] == 2:
                mine, give = attend(queries, keys, values, lens, starts[p] + jnp.stack([core, 1 - core]).astype(jnp.int32), seq_len)
            else:
                attn, = attend(queries, keys, values, lens, jnp.full((1,), starts[p], jnp.int32), seq_len)
                mine, give = rows_of(attn, core, seq_len // 2), rows_of(attn, 1 - core, seq_len // 2)
            lens = after(seq_lens, mine)
            heads = jnp.concatenate([mine, swap(give, sibling)], axis=1)
            if p >= 1:
                heads = after(heads, w_full)
            from_first = swap(heads, first_axis)
            from_second = swap(heads, second_axis)
            arrived.append([heads, from_first, from_second, swap(from_first, second_axis)])

        at_keep = bit_first ^ core

        def out_stage(p, places_after):
            rows = PIECES[p] * seq_len
            hidden, normed = project_out(arrived[p], w_full, x_rows, mlp_gain, places_after, starts[p] * seq_len)
            part = lambda row, col: lax.dynamic_slice(hidden, (row * (rows // 4), col * half), (rows // 4, half))
            take = swap(part(bit_first, 1 - core), sibling)
            normed_other = swap(normed, sibling)
            return (normed, normed_other), lambda: jnp.where(bit_first == core, part(bit_second, core), take).astype(F32)

        def place(p, y_rows, blocks):
            return place_rows(y_rows, blocks, starts[p] * seq_len // blocks.shape[1])

        def pair_sum(part_own, from_sibling, at, quarter):
            n = part_own.shape[0] // (2 if quarter is None else 4)
            offset = 0 if quarter is None else quarter * n
            own = lax.dynamic_slice_in_dim(part_own, at * (part_own.shape[0] // 2) + offset, n, 0)
            other = lax.dynamic_slice_in_dim(from_sibling, (1 - at) * (part_own.shape[0] // 2) + offset, n, 0)
            return own.astype(F32) + other.astype(F32)

        def second_stage(parts, got):
            n = got.shape[0] // 2
            send = pair_sum(*parts, at_keep, 1 - bit_second) + rows_of(got, 1 - bit_second, n)
            return send, swap(send, second_axis)

        def finish(residual, parts, got, got_second):
            n = got_second.shape[0]
            total = (pair_sum(*parts, at_keep, bit_second) + rows_of(got, bit_second, n)) + got_second
            mine = (residual() + total).astype(BF16)
            return mine, lax.all_gather(mine, "tp", axis=0)

        y_rows = jax.ShapeDtypeStruct(x_rows.shape, x_rows.dtype)
        normed_rows, residual = out_stage(0, after(places, lens))
        one = two = gathered = None
        for p in range(count):
            gated = gate_up(*normed_rows, w_gate, w_up)
            if one is not None:
                its_residual, parts, got = one
                got = after(got, gated)
                send, got_second = second_stage(parts, got)
                two = (its_residual, parts, got, got_second)
                gated = after(gated, send)
            part_other = jnp.dot(gated, down_other, preferred_element_type=F32).astype(BF16)
            from_sibling = swap(part_other, sibling)
            part_own = jnp.dot(after(gated, part_other), down_own, preferred_element_type=F32).astype(BF16)
            send = pair_sum(part_own, from_sibling, 1 - at_keep, None)
            one = (residual, (part_own, from_sibling), swap(send, first_axis))
            done = send
            if p + 1 < count:
                normed_rows, residual = out_stage(p + 1, after(places, send))
                done = normed_rows[0]
            if gathered is not None:
                y_rows = place(p - 2, y_rows, after(gathered, send))
                gathered = None
            if two is not None:
                its_residual, parts, got, got_second = two
                mine, gathered = finish(its_residual, parts, got, after(got_second, done))
                two = None
                if p + 1 < count:
                    normed_rows = (after(normed_rows[0], mine), normed_rows[1])
        its_residual, parts, got = one
        _, got_second = second_stage(parts, got)
        _, last = finish(its_residual, parts, got, got_second)
        y_rows = place(count - 2, y_rows, gathered)
        y_rows = place(count - 1, y_rows, last)
        return y_rows.reshape(x.shape), k_cache_out, v_cache_out

    cache_spec = P("dp", None, "tp", None)
    return jax.shard_map(layer_shard, mesh=mesh, in_specs=(P("dp", None, None), P("dp"), P(None, "tp"), P(None, "tp"), P(None, "tp"), P("tp", None), P(None, "tp"), P(None, "tp"), P("tp", None), P(), P(), cache_spec, cache_spec), out_specs=(P("dp", None, None), cache_spec, cache_spec), check_vma=False)
```

time: 1560 us -> 1440 us (0.923)
  Pallas kernels: 304 us -> 583 us
  matrix products: 389 us -> 130 us
  local copies, waits for them, and re-layouts: 212 us -> 30.7 us
  waiting for transfers between devices: 483 us -> 556 us
  other arithmetic: 133 us -> 82.9 us
  starting transfers between devices: 14.8 us -> 37.5 us
    ppermute x20 -> x45, waiting for transfers between devices: 238 us -> 526 us  [swap(): return lax.ppermute(value, 'tp', pairs)]
    pallas_call x4 -> x15, Pallas kernels: 50.6 us -> 336 us  [the longest x5 236 us: gate_up(): pl.pallas_call(functools.partial(gate_kernel, tiles), grid=(2 * tiles, hi...]
    dot_general x12 -> x5, matrix products: 325 us -> 63.7 us  [layer_shard(): jnp.dot(after(gated, part_other), down_own, preferred_element_type=F32)]
    all_gather x1, waiting for transfers between devices: 159 us -> 29.9 us  [layer_shard(): w_full = lax.all_gather(w_out, 'tp', axis=0, tiled=True)]
    all_gather x8 -> x5, waiting for transfers between devices: 85.2 us -> 0.01 us  [finish(): return (mine, lax.all_gather(mine, 'tp', axis=0))]
    transpose x8 -> x0, local copies, waits for them, and re-layouts: 47.5 us -> none  [layer_shard(): left = jnp.transpose(blocks[:, :, 0], (1, 0, 2, 3))]
    reshape x4 -> x0, local copies, waits for them, and re-layouts: 46 us -> none  [layer_shard(): hidden_parts = hidden.reshape(2, block, 2, half)]
    dynamic_slice x4 -> x7, local copies, waits for them, and re-layouts: 44.2 us -> 7.1 us  [the longest x5 6.98 us: out_stage(): lax.dynamic_slice(hidden, (row * (rows // 4), col * half), (rows // 4, ha...]
  transfers between devices with their start and end apart: 29 -> 51, of which waited for: 16 -> 23; matrix products, arithmetic and copies ran while one was open for 42% -> 14% of each run, Pallas kernels for 14% -> 32%
where the time goes in v2:
time: 1440 us; the launch traced here: 1430 us
  Pallas kernels  583 us (40%)
  waiting for transfers between devices  556 us (39%)
  matrix products  130 us (9%)
  other arithmetic  82.9 us (6%)
  starting transfers between devices  37.5 us (3%)
  local copies, waits for them, and re-layouts  30.7 us (2%)
  between operations  15.1 us (1%)
    ppermute x45, waiting for transfers between devices, swap(): return lax.ppermute(value, 'tp', pairs)  526 us
    pallas_call x5, Pallas kernels, gate_up(): pl.pallas_call(functools.partial(gate_kernel, tiles), grid=(2 * tiles, hi...  236 us
    pallas_call x5, Pallas kernels, project_out(): pl.pallas_call(out_kernel, grid_spec=pltpu.PrefetchScalarGridSpec(num_sca...  179 us
    pallas_call x1, Pallas kernels, project_qkv(): pl.pallas_call(functools.partial(qkv_kernel, tiles), grid_spec=pltpu.Pref...  68.5 us
    dot_general x5, matrix products, layer_shard(): jnp.dot(gated, down_other, preferred_element_type=F32).astype(BF16)  65.9 us
    dot_general x5, matrix products, layer_shard(): jnp.dot(after(gated, part_other), down_own, preferred_element_type=F32)  63.7 us
    pallas_call x5, Pallas kernels, place_rows(): pl.pallas_call(place_kernel, grid=(count,), in_specs=[pl.BlockSpec((1, ro...  50.1 us
    pallas_call x5, Pallas kernels, attend(): pl.pallas_call(attention_kernel, grid_spec=pltpu.PrefetchScalarGridSpec(n...  49.8 us
  transfers between devices with their start and end apart: 51, of which 23 were waited for; matrix products, arithmetic and copies ran while one was open for 14% of the time, Pallas kernels for 32%

profile of v2, /device:TPU:0, one launch (start us, length us, event | category | flops | bytes accessed | tf_op | source)
XLA Modules:
  0.0 1434.6 jit_solution(17380856369432547383)
XLA Ops:
  20.6 68.5 %shard_map.148 = (bf16[6144,512]{1,0:T(8,128)(2,1)}, bf16[6144,128]{1,0:T(8,128)(2,1)}, bf16[6144,128]{1,0:T(8,128)(2,1)}) custom-call(s32[8]{0:T(128)} %lens_ref.7, bf16[6144,4096]{1,0:T(8,128)(2,1)} %bitcast.36, bf16[1,4096]{1,0:T(2,128)(2,1)} %reshape.58.gain_ref, bf16[4096,512]{1,0:T(8,128)(2,1)} %wq_ref.1, bf16[4096,256]{1,0:T(8,128)(2,1)} %pad_maximum_fusion.wkv_ref, ...), custom_call_target="tpu_custom_call" | custom-call | flops 38654705664 | bytes 50331648 | tf_op jit(solution)/shard_map/pallas_call | solution.py:122
  105.6 32.9 %collective-permute-done.1.refs_1_ = bf16[384,1024]{1,0:T(8,128)(2,1)S(1)} collective-permute-done((bf16[384,1024]{1,0:T(8,128)(2,1)S(1)}, bf16[384,1024]{1,0:T(8,128)(2,1)S(1)}, u32[]{:S(2)}, u32[]{:S(2)}) %collective-permute-start.1) | collective-permute-done | bytes 786464 | tf_op jit(solution)/shard_map/ppermute | solution.py:243
  142.4 25.8 %collective-permute-done.3.refs_3_ = bf16[384,1024]{1,0:T(8,128)(2,1)} collective-permute-done((bf16[384,1024]{1,0:T(8,128)(2,1)S(1)}, bf16[384,1024]{1,0:T(8,128)(2,1)}, u32[]{:S(2)}, u32[]{:S(2)}) %collective-permute-start.3) | collective-permute-done | bytes 786464 | tf_op jit(solution)/shard_map/ppermute | solution.py:243
  168.1 29.9 %all-gather.12.cloned.1.call-done.refs_4_ = bf16[4096,4096]{1,0:T(8,128)(2,1)} async-done(((bf16[512,4096]{1,0:T(8,128)(2,1)}), bf16[4096,4096]{1,0:T(8,128)(2,1)}) %all-gather.12.cloned.1.call-update) | async-done | bytes 33554448 | tf_op jit(solution)/shard_map/all_gather | solution.py:257
  198.0 25.4 %shard_map.150 = (bf16[384,4096]{1,0:T(8,128)(2,1)}, bf16[384,4096]{1,0:T(8,128)(2,1)}) custom-call(s32[5]{0:T(128)} %stack.36.place_ref, bf16[384,1024]{1,0:T(8,128)(2,1)} %copy-done.13, bf16[384,1024]{1,0:T(8,128)(2,1)} %copy-done.21, bf16[384,1024]{1,0:T(8,128)(2,1)} %collective-permute-done.2.refs_2_, bf16[384,1024]{1,0:T(8,128)(2,1)} %collective-permute-done.3.refs_3_, ...), custom_call_target="tpu_custom_call" | custom-call | flops 12884901888 | bytes 67108864 | tf_op jit(solution)/shard_map/pallas_call | solution.py:156
  225.2 12.6 shard_map.152
  238.1 33.6 %shard_map.151 = bf16[768,1792]{1,0:T(8,128)(2,1)} custom-call(bf16[384,4096]{1,0:T(8,128)(2,1)} %get-tuple-element.60.mine_ref, bf16[384,4096]{1,0:T(8,128)(2,1)} %collective-permute-done.4.other_ref, bf16[4096,1792]{1,0:T(8,128)(2,1)} %gate_ref.9, bf16[4096,1792]{1,0:T(8,128)(2,1)} %up_ref.9), custom_call_target="tpu_custom_call" | custom-call | flops 22548578304 | bytes 12582912 | tf_op jit(solution)/shard_map/pallas_call | solution.py:195
  286.6 34.9 %collective-permute-done.7.refs_1_ = bf16[768,1024]{1,0:T(8,128)(2,1)} collective-permute-done((bf16[768,1024]{1,0:T(8,128)(2,1)}, bf16[768,1024]{1,0:T(8,128)(2,1)}, u32[]{:S(2)}, u32[]{:S(2)}) %collective-permute-start.7) | collective-permute-done | bytes 1572896 | tf_op jit(solution)/shard_map/ppermute | solution.py:243
  342.3 42.7 %shard_map.153 = (bf16[768,4096]{1,0:T(8,128)(2,1)}, bf16[768,4096]{1,0:T(8,128)(2,1)}) custom-call(s32[5]{0:T(128)} %stack.36.place_ref, bf16[768,1024]{1,0:T(8,128)(2,1)} %pad_maximum_fusion.1.refs_0_, bf16[768,1024]{1,0:T(8,128)(2,1)} %collective-permute-done.7.refs_1_, bf16[768,1024]{1,0:T(8,128)(2,1)} %copy-done.28, ...), custom_call_target="tpu_custom_call" | custom-call | flops 25769803776 | bytes 67108864 | tf_op jit(solution)/shard_map/pallas_call | solution.py:156
  395.5 55.4 %shard_map.154 = bf16[1536,1792]{1,0:T(8,128)(2,1)} custom-call(bf16[768,4096]{1,0:T(8,128)(2,1)} %get-tuple-element.67.mine_ref, bf16[768,4096]{1,0:T(8,128)(2,1)} %collective-permute-done.10.other_ref, bf16[4096,1792]{1,0:T(8,128)(2,1)} %gate_ref.9, bf16[4096,1792]{1,0:T(8,128)(2,1)} %up_ref.9), custom_call_target="tpu_custom_call" | custom-call | flops 45097156608 | bytes 25165824 | tf_op jit(solution)/shard_map/pallas_call | solution.py:195
  454.2 17.3 %convolution_convert_fusion.5 = bf16[1536,2048]{1,0:T(8,128)(2,1)} fusion(bf16[1536,1792]{1,0:T(8,128)(2,1)} %shard_map.154, bf16[1792,4096]{1,0:T(8,128)(2,1)} %param.21, s32[]{:T(128)S(6)} %select_n.196), kind=kOutput, calls=%fused_computation.5 | convolution fusion | flops 11277434880 | bytes 19136516 | tf_op jit(solution)/shard_map/dot_general | solution.py:329
  489.5 35.0 %collective-permute-done.14.refs_1_ = bf16[768,1024]{1,0:T(8,128)(2,1)} collective-permute-done((bf16[768,1024]{1,0:T(8,128)(2,1)}, bf16[768,1024]{1,0:T(8,128)(2,1)}, u32[]{:S(2)}, u32[]{:S(2)}) %collective-permute-start.14) | collective-permute-done | bytes 1572896 | tf_op jit(solution)/shard_map/ppermute | solution.py:243
  524.5 15.6 %convolution_convert_fusion.4 = bf16[1536,2048]{1,0:T(8,128)(2,1)S(1)} fusion(bf16[1536,1792]{1,0:T(8,128)(2,1)} %shard_map.154, bf16[1792,4096]{1,0:T(8,128)(2,1)} %param.21, s32[]{:T(128)S(6)} %select_n.197), kind=kOutput, calls=%fused_computation.4 | convolution fusion | flops 11277434880 | bytes 19136516 | tf_op jit(solution)/shard_map/dot_general | solution.py:331
  549.4 42.7 %shard_map.156 = (bf16[768,4096]{1,0:T(8,128)(2,1)}, bf16[768,4096]{1,0:T(8,128)(2,1)}) custom-call(s32[5]{0:T(128)} %stack.36.place_ref, bf16[768,1024]{1,0:T(8,128)(2,1)} %pad_maximum_fusion.2.refs_0_, bf16[768,1024]{1,0:T(8,128)(2,1)} %collective-permute-done.14.refs_1_, bf16[768,1024]{1,0:T(8,128)(2,1)} %copy-done.29, ...), custom_call_target="tpu_custom_call" | custom-call | flops 25769803776 | bytes 67108864 | tf_op jit(solution)/shard_map/pallas_call | solution.py:156
  597.2 32.0 %collective-permute-done.18 = f32[192,2048]{1,0:T(8,128)} collective-permute-done((f32[192,2048]{1,0:T(8,128)}, f32[192,2048]{1,0:T(8,128)}, u32[]{:S(2)}, u32[]{:S(2)}) %collective-permute-start.18) | collective-permute-done | bytes 1572896 | tf_op jit(solution)/shard_map/ppermute | solution.py:243
  633.5 55.4 %shard_map.157 = bf16[1536,1792]{1,0:T(8,128)(2,1)} custom-call(bf16[768,4096]{1,0:T(8,128)(2,1)} %get-tuple-element.79.mine_ref, bf16[768,4096]{1,0:T(8,128)(2,1)} %collective-permute-done.19.other_ref, bf16[4096,1792]{1,0:T(8,128)(2,1)} %gate_ref.9, bf16[4096,1792]{1,0:T(8,128)(2,1)} %up_ref.9), custom_call_target="tpu_custom_call" | custom-call | flops 45097156608 | bytes 25165824 | tf_op jit(solution)/shard_map/pallas_call | solution.py:195
  688.9 16.4 %collective-permute-done.20 = f32[768,2048]{1,0:T(8,128)} collective-permute-done((f32[768,2048]{1,0:T(8,128)}, f32[768,2048]{1,0:T(8,128)}, u32[]{:S(2)}, u32[]{:S(2)}) %collective-permute-start.20) | collective-permute-done | bytes 6291488 | tf_op jit(solution)/shard_map/ppermute | solution.py:243
  710.6 15.9 %convolution_convert_fusion.3 = bf16[1536,2048]{1,0:T(8,128)(2,1)} fusion(bf16[1536,1792]{1,0:T(8,128)(2,1)S(1)} %copy-done.30, bf16[1792,4096]{1,0:T(8,128)(2,1)} %param.21, s32[]{:T(128)S(6)} %select_n.196), kind=kOutput, calls=%fused_computation.3 | convolution fusion | flops 11277434880 | bytes 19136516 | tf_op jit(solution)/shard_map/dot_general | solution.py:329
  744.9 33.5 %collective-permute-done.23.refs_1_ = bf16[768,1024]{1,0:T(8,128)(2,1)} collective-permute-done((bf16[768,1024]{1,0:T(8,128)(2,1)S(1)}, bf16[768,1024]{1,0:T(8,128)(2,1)}, u32[]{:S(2)}, u32[]{:S(2)}) %collective-permute-start.23) | collective-permute-done | bytes 1572896 | tf_op jit(solution)/shard_map/ppermute | solution.py:243
  783.2 15.6 %convolution_convert_fusion.2 = bf16[1536,2048]{1,0:T(8,128)(2,1)S(1)} fusion(bf16[1536,1792]{1,0:T(8,128)(2,1)} %shard_map.157, bf16[1792,4096]{1,0:T(8,128)(2,1)} %param.21, s32[]{:T(128)S(6)} %select_n.197), kind=kOutput, calls=%fused_computation.2 | convolution fusion | flops 11277434880 | bytes 19136516 | tf_op jit(solution)/shard_map/dot_general | solution.py:331
  808.0 42.7 %shard_map.159 = (bf16[768,4096]{1,0:T(8,128)(2,1)}, bf16[768,4096]{1,0:T(8,128)(2,1)}) custom-call(s32[5]{0:T(128)} %stack.36.place_ref, bf16[768,1024]{1,0:T(8,128)(2,1)} %copy-done.19, bf16[768,1024]{1,0:T(8,128)(2,1)} %collective-permute-done.23.refs_1_, bf16[768,1024]{1,0:T(8,128)(2,1)} %copy-done.27, ...), custom_call_target="tpu_custom_call" | custom-call | flops 25769803776 | bytes 67108864 | tf_op jit(solution)/shard_map/pallas_call | solution.py:156
  862.3 57.0 %shard_map.160 = bf16[1536,1792]{1,0:T(8,128)(2,1)} custom-call(bf16[768,4096]{1,0:T(8,128)(2,1)} %get-tuple-element.91.mine_ref, bf16[768,4096]{1,0:T(8,128)(2,1)} %collective-permute-done.28.other_ref, bf16[4096,1792]{1,0:T(8,128)(2,1)} %gate_ref.9, bf16[4096,1792]{1,0:T(8,128)(2,1)} %up_ref.9), custom_call_target="tpu_custom_call" | custom-call | flops 45097156608 | bytes 25165824 | tf_op jit(solution)/shard_map/pallas_call | solution.py:195
  919.4 61.7 %collective-permute-done.29 = f32[768,2048]{1,0:T(8,128)} collective-permute-done((f32[768,2048]{1,0:T(8,128)}, f32[768,2048]{1,0:T(8,128)}, u32[]{:S(2)}, u32[]{:S(2)}) %collective-permute-start.29) | collective-permute-done | bytes 6291488 | tf_op jit(solution)/shard_map/ppermute | solution.py:243
  986.4 14.2 convolution_convert_fusion.1
  1013.9 17.6 %collective-permute-done.32.refs_1_ = bf16[384,1024]{1,0:T(8,128)(2,1)S(1)} collective-permute-done((bf16[384,1024]{1,0:T(8,128)(2,1)S(1)}, bf16[384,1024]{1,0:T(8,128)(2,1)S(1)}, u32[]{:S(2)}, u32[]{:S(2)}) %collective-permute-start.32) | collective-permute-done | bytes 786464 | tf_op jit(solution)/shard_map/ppermute | solution.py:243
  1036.2 15.6 %convolution_convert_fusion = bf16[1536,2048]{1,0:T(8,128)(2,1)S(1)} fusion(bf16[1536,1792]{1,0:T(8,128)(2,1)} %shard_map.160, bf16[1792,4096]{1,0:T(8,128)(2,1)} %param.21, s32[]{:T(128)S(6)} %select_n.197), kind=kOutput, calls=%fused_computation | convolution fusion | flops 11277434880 | bytes 19136516 | tf_op jit(solution)/shard_map/dot_general | solution.py:331
  1059.0 25.4 %shard_map.162 = (bf16[384,4096]{1,0:T(8,128)(2,1)}, bf16[384,4096]{1,0:T(8,128)(2,1)}) custom-call(s32[5]{0:T(128)} %stack.36.place_ref, bf16[384,1024]{1,0:T(8,128)(2,1)} %copy-done.14, bf16[384,1024]{1,0:T(8,128)(2,1)} %copy-done.22, bf16[384,1024]{1,0:T(8,128)(2,1)} %copy-done.23, bf16[384,1024]{1,0:T(8,128)(2,1)} %collective-permute-done.34.refs_3_, ...), custom_call_target="tpu_custom_call" | custom-call | flops 12884901888 | bytes 67108864 | tf_op jit(solution)/shard_map/pallas_call | solution.py:156
  1098.9 34.3 %shard_map.163 = bf16[768,1792]{1,0:T(8,128)(2,1)} custom-call(bf16[384,4096]{1,0:T(8,128)(2,1)} %get-tuple-element.102.mine_ref, bf16[384,4096]{1,0:T(8,128)(2,1)} %collective-permute-done.38.other_ref, bf16[4096,1792]{1,0:T(8,128)(2,1)} %gate_ref.9, bf16[4096,1792]{1,0:T(8,128)(2,1)} %up_ref.9), custom_call_target="tpu_custom_call" | custom-call | flops 22548578304 | bytes 12582912 | tf_op jit(solution)/shard_map/pallas_call | solution.py:195
  1133.2 80.3 %collective-permute-done.39 = f32[768,2048]{1,0:T(8,128)} collective-permute-done((f32[768,2048]{1,0:T(8,128)}, f32[768,2048]{1,0:T(8,128)}, u32[]{:S(2)}, u32[]{:S(2)}) %collective-permute-start.39) | collective-permute-done | bytes 6291488 | tf_op jit(solution)/shard_map/ppermute | solution.py:243
  1238.9 23.9 %collective-permute-done.44 = f32[384,2048]{1,0:T(8,128)S(1)} collective-permute-done((f32[384,2048]{1,0:T(8,128)S(1)}, f32[384,2048]{1,0:T(8,128)S(1)}, u32[]{:S(2)}, u32[]{:S(2)}) %collective-permute-start.44) | collective-permute-done | bytes 3145760 | tf_op jit(solution)/shard_map/ppermute | solution.py:243
  1270.1 80.1 %collective-permute-done.41 = f32[384,2048]{1,0:T(8,128)S(1)} collective-permute-done((f32[384,2048]{1,0:T(8,128)}, f32[384,2048]{1,0:T(8,128)S(1)}, u32[]{:S(2)}, u32[]{:S(2)}) %collective-permute-start.41) | collective-permute-done | bytes 3145760 | tf_op jit(solution)/shard_map/ppermute | solution.py:243
  1354.4 17.9 %collective-permute-done.42 = f32[192,2048]{1,0:T(8,128)S(1)} collective-permute-done((f32[192,2048]{1,0:T(8,128)S(1)}, f32[192,2048]{1,0:T(8,128)S(1)}, u32[]{:S(2)}, u32[]{:S(2)}) %collective-permute-start.42) | collective-permute-done | bytes 1572896 | tf_op jit(solution)/shard_map/ppermute | solution.py:243
  (225 shorter events, 307.9 us)
Async XLA Ops:
  7.2 190.8 %all-gather.12.cloned.1.call-start = ((), (), s32[]{:S(2)}) async-start(), calls=%async_computation | async-start | bytes 37748736 | tf_op jit(solution)/shard_map/all_gather | solution.py:257
  12.9 1364.6 %all-gather.22.cloned.1.call-start = ((), (), s32[]{:S(2)}) async-start(), calls=%async_computation.5 | async-start | bytes 7077888 | tf_op jit(solution)/shard_map/all_gather | solution.py:316
  100.8 37.7 %collective-permute-start.1 = (bf16[384,1024]{1,0:T(8,128)(2,1)S(1)}, bf16[384,1024]{1,0:T(8,128)(2,1)S(1)}, u32[]{:S(2)}, u32[]{:S(2)}) collective-permute-start(bf16[384,1024]{1,0:T(8,128)(2,1)S(1)} %pad_maximum_fusion.4.refs_0_), channel_id=1, source_target_pairs={{0,2},{1,5},{2,0},{3,7},{4,6},{5,1},{6,4},{7,3},{8,10},{9,13},{10,... | collective-permute-start | bytes 2359304 | tf_op jit(solution)/shard_map/ppermute | solution.py:243
  103.5 38.8 %collective-permute-start.2 = (bf16[384,1024]{1,0:T(8,128)(2,1)S(1)}, bf16[384,1024]{1,0:T(8,128)(2,1)}, u32[]{:S(2)}, u32[]{:S(2)}) collective-permute-start(bf16[384,1024]{1,0:T(8,128)(2,1)S(1)} %pad_maximum_fusion.4.refs_0_), channel_id=1, source_target_pairs={{0,4},{1,3},{2,6},{3,1},{4,0},{5,7},{6,2},{7,5},{8,12},{9,11},{10,... | collective-permute-start | bytes 2359304 | tf_op jit(solution)/shard_map/ppermute | solution.py:243
  237.8 44.3 %collective-permute-start.6 = (bf16[768,512]{1,0:T(8,128)(2,1)}, bf16[768,512]{1,0:T(8,128)(2,1)}, u32[]{:S(2)}, u32[]{:S(2)}) collective-permute-start(bf16[768,512]{1,0:T(8,128)(2,1)} %get-tuple-element.65), channel_id=1, source_target_pairs={{0,1},{1,0},{2,3},{3,2},{4,5},{5,4},{6,7},{7,6},{8,9},{9,8},{10,11... | collective-permute-start | bytes 2359304 | tf_op jit(solution)/shard_map/ppermute | solution.py:243
  281.8 48.9 %collective-permute-start.5 = (bf16[768,2048]{1,0:T(8,128)(2,1)}, bf16[768,2048]{1,0:T(8,128)(2,1)}, u32[]{:S(2)}, u32[]{:S(2)}) collective-permute-start(bf16[768,2048]{1,0:T(8,128)(2,1)} %fusion.14), channel_id=1, source_target_pairs={{0,1},{1,0},{2,3},{3,2},{4,5},{5,4},{6,7},{7,6},{8,9},{9,8},{10,11... | collective-permute-start | bytes 9437192 | tf_op jit(solution)/shard_map/ppermute | solution.py:243
  284.5 37.0 %collective-permute-start.7 = (bf16[768,1024]{1,0:T(8,128)(2,1)}, bf16[768,1024]{1,0:T(8,128)(2,1)}, u32[]{:S(2)}, u32[]{:S(2)}) collective-permute-start(bf16[768,1024]{1,0:T(8,128)(2,1)} %pad_maximum_fusion.1.refs_0_), channel_id=1, source_target_pairs={{0,2},{1,5},{2,0},{3,7},{4,6},{5,1},{6,4},{7,3},{8,10},{9,13},{10,... | collective-permute-start | bytes 4718600 | tf_op jit(solution)/shard_map/ppermute | solution.py:243
  286.1 49.4 %collective-permute-start.8 = (bf16[768,1024]{1,0:T(8,128)(2,1)}, bf16[768,1024]{1,0:T(8,128)(2,1)S(1)}, u32[]{:S(2)}, u32[]{:S(2)}) collective-permute-start(bf16[768,1024]{1,0:T(8,128)(2,1)} %pad_maximum_fusion.1.refs_0_), channel_id=1, source_target_pairs={{0,4},{1,3},{2,6},{3,1},{4,0},{5,7},{6,2},{7,5},{8,12},{9,11},{10,... | collective-permute-start | bytes 4718600 | tf_op jit(solution)/shard_map/ppermute | solution.py:243
  385.1 65.8 %collective-permute-start.11 = (f32[384,2048]{1,0:T(8,128)}, f32[384,2048]{1,0:T(8,128)}, u32[]{:S(2)}, u32[]{:S(2)}) collective-permute-start(f32[384,2048]{1,0:T(8,128)} %convert_add_fusion.4), channel_id=1, source_target_pairs={{0,2},{1,5},{2,0},{3,7},{4,6},{5,1},{6,4},{7,3},{8,10},{9,13},{10,... | collective-permute-start | bytes 9437192 | tf_op jit(solution)/shard_map/ppermute | solution.py:243
  471.5 68.5 %collective-permute-start.12 = (bf16[1536,2048]{1,0:T(8,128)(2,1)}, bf16[1536,2048]{1,0:T(8,128)(2,1)}, u32[]{:S(2)}, u32[]{:S(2)}) collective-permute-start(bf16[1536,2048]{1,0:T(8,128)(2,1)} %convolution_convert_fusion.5), channel_id=1, source_target_pairs={{0,1},{1,0},{2,3},{3,2},{4,5},{5,4},{6,7},{7,6},{8,9},{9,8},{10,11... | collective-permute-start | bytes 18874376 | tf_op jit(solution)/shard_map/ppermute | solution.py:243
  487.3 37.1 %collective-permute-start.14 = (bf16[768,1024]{1,0:T(8,128)(2,1)}, bf16[768,1024]{1,0:T(8,128)(2,1)}, u32[]{:S(2)}, u32[]{:S(2)}) collective-permute-start(bf16[768,1024]{1,0:T(8,128)(2,1)} %pad_maximum_fusion.2.refs_0_), channel_id=1, source_target_pairs={{0,2},{1,5},{2,0},{3,7},{4,6},{5,1},{6,4},{7,3},{8,10},{9,13},{10,... | collective-permute-start | bytes 4718600 | tf_op jit(solution)/shard_map/ppermute | solution.py:243
  489.0 59.2 %collective-permute-start.15 = (bf16[768,1024]{1,0:T(8,128)(2,1)}, bf16[768,1024]{1,0:T(8,128)(2,1)S(1)}, u32[]{:S(2)}, u32[]{:S(2)}) collective-permute-start(bf16[768,1024]{1,0:T(8,128)(2,1)} %pad_maximum_fusion.2.refs_0_), channel_id=1, source_target_pairs={{0,4},{1,3},{2,6},{3,1},{4,0},{5,7},{6,2},{7,5},{8,12},{9,11},{10,... | collective-permute-start | bytes 4718600 | tf_op jit(solution)/shard_map/ppermute | solution.py:243
  592.1 41.4 %collective-permute-start.19 = (bf16[768,4096]{1,0:T(8,128)(2,1)}, bf16[768,4096]{1,0:T(8,128)(2,1)}, u32[]{:S(2)}, u32[]{:S(2)}) collective-permute-start(bf16[768,4096]{1,0:T(8,128)(2,1)} %get-tuple-element.79.mine_ref), channel_id=1, source_target_pairs={{0,1},{1,0},{2,3},{3,2},{4,5},{5,4},{6,7},{7,6},{8,9},{9,8},{10,11... | collective-permute-start | bytes 18874376 | tf_op jit(solution)/shard_map/ppermute | solution.py:243
  592.5 36.7 %collective-permute-start.18 = (f32[192,2048]{1,0:T(8,128)}, f32[192,2048]{1,0:T(8,128)}, u32[]{:S(2)}, u32[]{:S(2)}) collective-permute-start(f32[192,2048]{1,0:T(8,128)} %dynamic-slice_add_fusion.4), channel_id=1, source_target_pairs={{0,4},{1,3},{2,6},{3,1},{4,0},{5,7},{6,2},{7,5},{8,12},{9,11},{10,... | collective-permute-start | bytes 4718600 | tf_op jit(solution)/shard_map/ppermute | solution.py:243
  594.2 111.1 %collective-permute-start.20 = (f32[768,2048]{1,0:T(8,128)}, f32[768,2048]{1,0:T(8,128)}, u32[]{:S(2)}, u32[]{:S(2)}) collective-permute-start(f32[768,2048]{1,0:T(8,128)} %convert_add_fusion.2), channel_id=1, source_target_pairs={{0,2},{1,5},{2,0},{3,7},{4,6},{5,1},{6,4},{7,3},{8,10},{9,13},{10,... | collective-permute-start | bytes 18874376 | tf_op jit(solution)/shard_map/ppermute | solution.py:243
  633.4 752.0 %all-gather.20.cloned.1.call-start = ((), (), s32[]{:S(2)}) async-start(), calls=%async_computation.4 | async-start | bytes 14155776 | tf_op jit(solution)/shard_map/all_gather | solution.py:316
  726.5 72.2 %collective-permute-start.21 = (bf16[1536,2048]{1,0:T(8,128)(2,1)}, bf16[1536,2048]{1,0:T(8,128)(2,1)}, u32[]{:S(2)}, u32[]{:S(2)}) collective-permute-start(bf16[1536,2048]{1,0:T(8,128)(2,1)} %convolution_convert_fusion.3), channel_id=1, source_target_pairs={{0,1},{1,0},{2,3},{3,2},{4,5},{5,4},{6,7},{7,6},{8,9},{9,8},{10,11... | collective-permute-start | bytes 18874376 | tf_op jit(solution)/shard_map/ppermute | solution.py:243
  741.6 36.8 %collective-permute-start.23 = (bf16[768,1024]{1,0:T(8,128)(2,1)S(1)}, bf16[768,1024]{1,0:T(8,128)(2,1)}, u32[]{:S(2)}, u32[]{:S(2)}) collective-permute-start(bf16[768,1024]{1,0:T(8,128)(2,1)S(1)} %pad_maximum_fusion.3.refs_0_), channel_id=1, source_target_pairs={{0,2},{1,5},{2,0},{3,7},{4,6},{5,1},{6,4},{7,3},{8,10},{9,13},{10,... | collective-permute-start | bytes 4718600 | tf_op jit(solution)/shard_map/ppermute | solution.py:243
  743.0 63.9 %collective-permute-start.24 = (bf16[768,1024]{1,0:T(8,128)(2,1)S(1)}, bf16[768,1024]{1,0:T(8,128)(2,1)S(1)}, u32[]{:S(2)}, u32[]{:S(2)}) collective-permute-start(bf16[768,1024]{1,0:T(8,128)(2,1)S(1)} %pad_maximum_fusion.3.refs_0_), channel_id=1, source_target_pairs={{0,4},{1,3},{2,6},{3,1},{4,0},{5,7},{6,2},{7,5},{8,12},{9,11},{10,... | collective-permute-start | bytes 4718600 | tf_op jit(solution)/shard_map/ppermute | solution.py:243
  782.7 69.5 %collective-permute-start.26 = (bf16[384,2048]{1,0:T(8,128)(2,1)}, bf16[384,2048]{1,0:T(8,128)(2,1)}, u32[]{:S(2)}, u32[]{:S(2)}) collective-permute-start(bf16[384,2048]{1,0:T(8,128)(2,1)} %dynamic_slice.190), channel_id=1, source_target_pairs={{0,1},{1,0},{2,3},{3,2},{4,5},{5,4},{6,7},{7,6},{8,9},{9,8},{10,11... | collective-permute-start | bytes 4718600 | tf_op jit(solution)/shard_map/ppermute | solution.py:243
  782.7 69.5 %collective-permute-start.27 = (f32[384,2048]{1,0:T(8,128)}, f32[384,2048]{1,0:T(8,128)}, u32[]{:S(2)}, u32[]{:S(2)}) collective-permute-start(f32[384,2048]{1,0:T(8,128)} %dynamic-slice_add_fusion.2), channel_id=1, source_target_pairs={{0,4},{1,3},{2,6},{3,1},{4,0},{5,7},{6,2},{7,5},{8,12},{9,11},{10,... | collective-permute-start | bytes 9437192 | tf_op jit(solution)/shard_map/ppermute | solution.py:243
  859.2 537.6 %all-gather.18.cloned.1.call-start = ((), (), s32[]{:S(2)}) async-start(), calls=%async_computation.3 | async-start | bytes 14155776 | tf_op jit(solution)/shard_map/all_gather | solution.py:316
  859.3 121.9 %collective-permute-start.29 = (f32[768,2048]{1,0:T(8,128)}, f32[768,2048]{1,0:T(8,128)}, u32[]{:S(2)}, u32[]{:S(2)}) collective-permute-start(f32[768,2048]{1,0:T(8,128)} %convert_add_fusion.1), channel_id=1, source_target_pairs={{0,2},{1,5},{2,0},{3,7},{4,6},{5,1},{6,4},{7,3},{8,10},{9,13},{10,... | collective-permute-start | bytes 18874376 | tf_op jit(solution)/shard_map/ppermute | solution.py:243
  1000.7 51.1 %collective-permute-start.30 = (bf16[1536,2048]{1,0:T(8,128)(2,1)S(1)}, bf16[1536,2048]{1,0:T(8,128)(2,1)S(1)}, u32[]{:S(2)}, u32[]{:S(2)}) collective-permute-start(bf16[1536,2048]{1,0:T(8,128)(2,1)S(1)} %convolution_convert_fusion.1), channel_id=1, source_target_pairs={{0,1},{1,0},{2,3},{3,2},{4,5},{5,4},{6,7},{7,6},{8,9},{9,8},{10,11... | collective-permute-start | bytes 18874376 | tf_op jit(solution)/shard_map/ppermute | solution.py:243
  1012.3 45.8 %collective-permute-start.33 = (bf16[384,1024]{1,0:T(8,128)(2,1)S(1)}, bf16[384,1024]{1,0:T(8,128)(2,1)S(1)}, u32[]{:S(2)}, u32[]{:S(2)}) collective-permute-start(bf16[384,1024]{1,0:T(8,128)(2,1)S(1)} %pad_maximum_fusion.5.refs_0_), channel_id=1, source_target_pairs={{0,4},{1,3},{2,6},{3,1},{4,0},{5,7},{6,2},{7,5},{8,12},{9,11},{10,... | collective-permute-start | bytes 2359304 | tf_op jit(solution)/shard_map/ppermute | solution.py:243
  1034.5 50.0 %collective-permute-start.36 = (bf16[384,2048]{1,0:T(8,128)(2,1)}, bf16[384,2048]{1,0:T(8,128)(2,1)}, u32[]{:S(2)}, u32[]{:S(2)}) collective-permute-start(bf16[384,2048]{1,0:T(8,128)(2,1)} %dynamic_slice.204), channel_id=1, source_target_pairs={{0,1},{1,0},{2,3},{3,2},{4,5},{5,4},{6,7},{7,6},{8,9},{9,8},{10,11... | collective-permute-start | bytes 4718600 | tf_op jit(solution)/shard_map/ppermute | solution.py:243
  1034.5 50.0 %collective-permute-start.37 = (f32[384,2048]{1,0:T(8,128)}, f32[384,2048]{1,0:T(8,128)}, u32[]{:S(2)}, u32[]{:S(2)}) collective-permute-start(f32[384,2048]{1,0:T(8,128)} %dynamic-slice_add_fusion.1), channel_id=1, source_target_pairs={{0,4},{1,3},{2,6},{3,1},{4,0},{5,7},{6,2},{7,5},{8,12},{9,11},{10,... | collective-permute-start | bytes 9437192 | tf_op jit(solution)/shard_map/ppermute | solution.py:243
  1091.5 316.8 %all-gather.16.cloned.1.call-start = ((), (), s32[]{:S(2)}) async-start(), calls=%async_computation.2 | async-start | bytes 14155776 | tf_op jit(solution)/shard_map/all_gather | solution.py:316
  1091.5 121.9 %collective-permute-start.39 = (f32[768,2048]{1,0:T(8,128)}, f32[768,2048]{1,0:T(8,128)}, u32[]{:S(2)}, u32[]{:S(2)}) collective-permute-start(f32[768,2048]{1,0:T(8,128)} %convert_add_fusion), channel_id=1, source_target_pairs={{0,2},{1,5},{2,0},{3,7},{4,6},{5,1},{6,4},{7,3},{8,10},{9,13},{10,... | collective-permute-start | bytes 18874376 | tf_op jit(solution)/shard_map/ppermute | solution.py:243
  1225.4 37.3 %collective-permute-start.44 = (f32[384,2048]{1,0:T(8,128)S(1)}, f32[384,2048]{1,0:T(8,128)S(1)}, u32[]{:S(2)}, u32[]{:S(2)}) collective-permute-start(f32[384,2048]{1,0:T(8,128)S(1)} %dynamic-slice_add_fusion), channel_id=1, source_target_pairs={{0,4},{1,3},{2,6},{3,1},{4,0},{5,7},{6,2},{7,5},{8,12},{9,11},{10,... | collective-permute-start | bytes 9437192 | tf_op jit(solution)/shard_map/ppermute | solution.py:243
  1268.5 151.2 %all-gather.14.cloned.1.call-start = ((), (), s32[]{:S(2)}) async-start(), calls=%async_computation.1 | async-start | bytes 7077888 | tf_op jit(solution)/shard_map/all_gather | solution.py:316
  1268.7 81.4 %collective-permute-start.41 = (f32[384,2048]{1,0:T(8,128)}, f32[384,2048]{1,0:T(8,128)S(1)}, u32[]{:S(2)}, u32[]{:S(2)}) collective-permute-start(f32[384,2048]{1,0:T(8,128)} %convert_add_fusion.3), channel_id=1, source_target_pairs={{0,2},{1,5},{2,0},{3,7},{4,6},{5,1},{6,4},{7,3},{8,10},{9,13},{10,... | collective-permute-start | bytes 9437192 | tf_op jit(solution)/shard_map/ppermute | solution.py:243
  (54 other events, 1067.9 us)
Sparse Core Ops, SparseCore 0:
  13.0 184.9 all-gather.11
  633.5 57.1 all-gather.21
  859.3 94.0 all-gather.19
  1091.6 94.5 all-gather.17
  1268.6 93.7 all-gather.15
  1375.3 43.2 all-gather.13

commit v3 on v2

--- a/solution.py
+++ b/solution.py
@@ -75,29 +75,25 @@
 
 
 def out_kernel(place_ref, *refs):
-    pairs, (w_ref, x_ref, gain_ref, h_ref, n_ref, total) = refs[:-6], refs[-6:]
+    pairs, (w_ref, x_ref, gain_ref, h_ref, n_ref, hidden) = refs[:-6], refs[-6:]
     step = pl.program_id(0)
     core = place_ref[0]
-    depth = w_ref.shape[0] // 2
-    tile = x_ref.shape[0]
-    at_rows = pl.ds(pl.multiple_of(pl.program_id(1) * tile, tile), tile)
-    cols = 1024
-
+    depth = w_ref.shape[0] // (2 * len(pairs))
+    rows, cols = x_ref.shape
+    total = None
     for which, o_ref in enumerate(pairs):
-        @pl.when(step == which)
-        def _():
-            for col in range(0, total.shape[1], cols):
-                at = slice(col, col + cols)
-                own = jnp.dot(o_ref[:, :depth], w_ref[pl.ds(pl.multiple_of(core * depth, depth), depth), at], preferred_element_type=F32).astype(BF16)
-                other = jnp.dot(o_ref[:, depth:], w_ref[pl.ds(pl.multiple_of((1 - core) * depth, depth), depth), at], preferred_element_type=F32).astype(BF16)
-                both = own.astype(F32) + other.astype(F32)
-                total[at_rows, at] = both if which == 0 else total[at_rows, at] + both
+        for k, owner in enumerate((core, 1 - core)):
+            group = 2 * place_ref[1 + which] + owner
+            part = jnp.dot(o_ref[:, k * depth:(k + 1) * depth], w_ref[pl.ds(pl.multiple_of(group * depth, depth), depth), :], preferred_element_type=F32).astype(BF16)
+            total = part.astype(F32) if total is None else total + part.astype(F32)
+    h = (x_ref[...].astype(F32) + total).astype(BF16)
+    h_ref[...] = h
+    hidden[:, pl.ds(pl.multiple_of(step * cols, cols), cols)] = h
 
     @pl.when(step == pl.num_programs(0) - 1)
     def _():
-        hidden = (x_ref[...].astype(F32) + total[at_rows, :]).astype(BF16)
-        h_ref[...] = hidden
-        n_ref[...] = rms_rows(hidden, gain_ref[...])
+        for row in range(0, rows, 128):
+            n_ref[row:row + 128, :] = rms_rows(hidden[row:row + 128, :], gain_ref[...])
 
 
 def rope_tables(seq_len, head):
@@ -150,19 +146,17 @@
 def project_out(pairs, w_full, x_rows, gain, places, first):
     rows, pair_cols = pairs[0].shape
     width = w_full.shape[1]
-    tile = 384
-    last = len(pairs) - 1
-    row_block = pl.BlockSpec((tile, width), lambda i, r, c: (jnp.where(i == last, r, 0), 0))
+    cols = 512
     return pl.pallas_call(
         out_kernel,
         grid_spec=pltpu.PrefetchScalarGridSpec(
-            num_scalar_prefetch=1, grid=(len(pairs), rows // tile),
-            in_specs=[pl.BlockSpec((tile, pair_cols), lambda i, r, c, j=j: (jnp.where(i == j, r, 0 if rows == tile else jnp.where(i < j, 0, rows // tile - 1)), 0)) for j in range(len(pairs))]
-                     + [pl.BlockSpec((pair_cols, width), lambda i, r, c: (c[1 + i], 0)),
-                        pl.BlockSpec((tile, width), lambda i, r, c: ((first + c[0] * rows) // tile + jnp.where(i == last, r, 0), 0)),
-                        pl.BlockSpec((1, width), lambda i, r, c: (0, 0))],
-            out_specs=[row_block, row_block],
-            scratch_shapes=[pltpu.VMEM((rows, width), F32)]),
+            num_scalar_prefetch=1, grid=(width // cols,),
+            in_specs=[pl.BlockSpec((rows, pair_cols), lambda n, c: (0, 0))] * len(pairs)
+                     + [pl.BlockSpec((width, cols), lambda n, c: (0, n)),
+                        pl.BlockSpec((rows, cols), lambda n, c: (first // rows + c[0], n)),
+                        pl.BlockSpec((1, width), lambda n, c: (0, 0))],
+            out_specs=[pl.BlockSpec((rows, cols), lambda n, c: (0, n)), pl.BlockSpec((rows, width), lambda n, c: (0, 0))],
+            scratch_shapes=[pltpu.VMEM((rows, width), BF16)]),
         out_shape=[jax.ShapeDtypeStruct((rows, width), BF16)] * 2,
         compiler_params=pltpu.CompilerParams(**vmem_limit(62)),
         cost_estimate=pl.CostEstimate(flops=2 * rows * width * len(pairs) * pair_cols, bytes_accessed=4 * width * width, transcendentals=0),

time: 1440 us -> 1440 us (level)
  no operation moved by 1% of the time
where the time goes in v3:
time: 1440 us; the launch traced here: 1430 us
  Pallas kernels  576 us (40%)
  waiting for transfers between devices  555 us (39%)
  matrix products  130 us (9%)
  other arithmetic  82.9 us (6%)
  starting transfers between devices  37.1 us (3%)
  local copies, waits for them, and re-layouts  30.7 us (2%)
  between operations  15.3 us (1%)
    ppermute x45, waiting for transfers between devices, swap(): return lax.ppermute(value, 'tp', pairs)  525 us
    pallas_call x5, Pallas kernels, gate_up(): pl.pallas_call(functools.partial(gate_kernel, tiles), grid=(2 * tiles, hi...  236 us
    pallas_call x5, Pallas kernels, project_out(): pl.pallas_call(out_kernel, grid_spec=pltpu.PrefetchScalarGridSpec(num_sca...  171 us
    pallas_call x1, Pallas kernels, project_qkv(): pl.pallas_call(functools.partial(qkv_kernel, tiles), grid_spec=pltpu.Pref...  68.6 us
    dot_general x5, matrix products, layer_shard(): jnp.dot(gated, down_other, preferred_element_type=F32).astype(BF16)  66.1 us
    dot_general x5, matrix products, layer_shard(): jnp.dot(after(gated, part_other), down_own, preferred_element_type=F32)  64.1 us
    pallas_call x5, Pallas kernels, attend(): pl.pallas_call(attention_kernel, grid_spec=pltpu.PrefetchScalarGridSpec(n...  50.1 us
    pallas_call x5, Pallas kernels, place_rows(): pl.pallas_call(place_kernel, grid=(count,), in_specs=[pl.BlockSpec((1, ro...  50 us
  transfers between devices with their start and end apart: 51, of which 23 were waited for; matrix products, arithmetic and copies ran while one was open for 14% of the time, Pallas kernels for 32%

profile of v3, /device:TPU:0, one launch (start us, length us, event | category | flops | bytes accessed | tf_op | source)
XLA Modules:
  0.0 1427.1 jit_solution(1560718447004314438)
XLA Ops:
  20.6 68.6 %shard_map.148 = (bf16[6144,512]{1,0:T(8,128)(2,1)}, bf16[6144,128]{1,0:T(8,128)(2,1)}, bf16[6144,128]{1,0:T(8,128)(2,1)}) custom-call(s32[8]{0:T(128)} %lens_ref.7, bf16[6144,4096]{1,0:T(8,128)(2,1)} %bitcast.36, bf16[1,4096]{1,0:T(2,128)(2,1)} %reshape.58.gain_ref, bf16[4096,512]{1,0:T(8,128)(2,1)} %wq_ref.1, bf16[4096,256]{1,0:T(8,128)(2,1)} %pad_maximum_fusion.wkv_ref, ...), custom_call_target="tpu_custom_call" | custom-call | flops 38654705664 | bytes 50331648 | tf_op jit(solution)/shard_map/pallas_call | solution.py:118
  105.7 32.9 %collective-permute-done.1.refs_1_ = bf16[384,1024]{1,0:T(8,128)(2,1)S(1)} collective-permute-done((bf16[384,1024]{1,0:T(8,128)(2,1)S(1)}, bf16[384,1024]{1,0:T(8,128)(2,1)S(1)}, u32[]{:S(2)}, u32[]{:S(2)}) %collective-permute-start.1) | collective-permute-done | bytes 786464 | tf_op jit(solution)/shard_map/ppermute | solution.py:237
  142.2 25.8 %collective-permute-done.3.refs_3_ = bf16[384,1024]{1,0:T(8,128)(2,1)} collective-permute-done((bf16[384,1024]{1,0:T(8,128)(2,1)S(1)}, bf16[384,1024]{1,0:T(8,128)(2,1)}, u32[]{:S(2)}, u32[]{:S(2)}) %collective-permute-start.3) | collective-permute-done | bytes 786464 | tf_op jit(solution)/shard_map/ppermute | solution.py:237
  168.0 30.1 %all-gather.12.cloned.1.call-done.refs_4_ = bf16[4096,4096]{1,0:T(8,128)(2,1)} async-done(((bf16[512,4096]{1,0:T(8,128)(2,1)}), bf16[4096,4096]{1,0:T(8,128)(2,1)}) %all-gather.12.cloned.1.call-update) | async-done | bytes 33554448 | tf_op jit(solution)/shard_map/all_gather | solution.py:251
  198.1 24.5 %shard_map.150 = (bf16[384,4096]{1,0:T(8,128)(2,1)}, bf16[384,4096]{1,0:T(8,128)(2,1)}) custom-call(s32[5]{0:T(128)} %stack.36.place_ref, bf16[384,1024]{1,0:T(8,128)(2,1)} %copy-done.13, bf16[384,1024]{1,0:T(8,128)(2,1)} %copy-done.21, bf16[384,1024]{1,0:T(8,128)(2,1)} %collective-permute-done.2.refs_2_, bf16[384,1024]{1,0:T(8,128)(2,1)} %collective-permute-done.3.refs_3_, ...), custom_call_target="tpu_custom_call" | custom-call | flops 12884901888 | bytes 67108864 | tf_op jit(solution)/shard_map/pallas_call | solution.py:150
  224.3 12.8 shard_map.152
  237.3 33.6 %shard_map.151 = bf16[768,1792]{1,0:T(8,128)(2,1)} custom-call(bf16[384,4096]{1,0:T(8,128)(2,1)} %get-tuple-element.60.mine_ref, bf16[384,4096]{1,0:T(8,128)(2,1)} %collective-permute-done.4.other_ref, bf16[4096,1792]{1,0:T(8,128)(2,1)} %gate_ref.9, bf16[4096,1792]{1,0:T(8,128)(2,1)} %up_ref.9), custom_call_target="tpu_custom_call" | custom-call | flops 22548578304 | bytes 12582912 | tf_op jit(solution)/shard_map/pallas_call | solution.py:189
  285.8 34.9 %collective-permute-done.7.refs_1_ = bf16[768,1024]{1,0:T(8,128)(2,1)} collective-permute-done((bf16[768,1024]{1,0:T(8,128)(2,1)}, bf16[768,1024]{1,0:T(8,128)(2,1)}, u32[]{:S(2)}, u32[]{:S(2)}) %collective-permute-start.7) | collective-permute-done | bytes 1572896 | tf_op jit(solution)/shard_map/ppermute | solution.py:237
  341.5 40.3 %shard_map.153 = (bf16[768,4096]{1,0:T(8,128)(2,1)}, bf16[768,4096]{1,0:T(8,128)(2,1)}) custom-call(s32[5]{0:T(128)} %stack.36.place_ref, bf16[768,1024]{1,0:T(8,128)(2,1)} %pad_maximum_fusion.1.refs_0_, bf16[768,1024]{1,0:T(8,128)(2,1)} %collective-permute-done.7.refs_1_, bf16[768,1024]{1,0:T(8,128)(2,1)} %copy-done.28, ...), custom_call_target="tpu_custom_call" | custom-call | flops 25769803776 | bytes 67108864 | tf_op jit(solution)/shard_map/pallas_call | solution.py:150
  392.3 55.5 %shard_map.154 = bf16[1536,1792]{1,0:T(8,128)(2,1)} custom-call(bf16[768,4096]{1,0:T(8,128)(2,1)} %get-tuple-element.67.mine_ref, bf16[768,4096]{1,0:T(8,128)(2,1)} %collective-permute-done.10.other_ref, bf16[4096,1792]{1,0:T(8,128)(2,1)} %gate_ref.9, bf16[4096,1792]{1,0:T(8,128)(2,1)} %up_ref.9), custom_call_target="tpu_custom_call" | custom-call | flops 45097156608 | bytes 25165824 | tf_op jit(solution)/shard_map/pallas_call | solution.py:189
  451.1 17.3 %convolution_convert_fusion.5 = bf16[1536,2048]{1,0:T(8,128)(2,1)} fusion(bf16[1536,1792]{1,0:T(8,128)(2,1)} %shard_map.154, bf16[1792,4096]{1,0:T(8,128)(2,1)} %param.21, s32[]{:T(128)S(6)} %select_n.196), kind=kOutput, calls=%fused_computation.5 | convolution fusion | flops 11277434880 | bytes 19136516 | tf_op jit(solution)/shard_map/dot_general | solution.py:323
  486.4 35.0 %collective-permute-done.14.refs_1_ = bf16[768,1024]{1,0:T(8,128)(2,1)} collective-permute-done((bf16[768,1024]{1,0:T(8,128)(2,1)}, bf16[768,1024]{1,0:T(8,128)(2,1)}, u32[]{:S(2)}, u32[]{:S(2)}) %collective-permute-start.14) | collective-permute-done | bytes 1572896 | tf_op jit(solution)/shard_map/ppermute | solution.py:237
  521.5 15.6 %convolution_convert_fusion.4 = bf16[1536,2048]{1,0:T(8,128)(2,1)S(1)} fusion(bf16[1536,1792]{1,0:T(8,128)(2,1)} %shard_map.154, bf16[1792,4096]{1,0:T(8,128)(2,1)} %param.21, s32[]{:T(128)S(6)} %select_n.197), kind=kOutput, calls=%fused_computation.4 | convolution fusion | flops 11277434880 | bytes 19136516 | tf_op jit(solution)/shard_map/dot_general | solution.py:325
  546.3 40.7 %shard_map.156 = (bf16[768,4096]{1,0:T(8,128)(2,1)}, bf16[768,4096]{1,0:T(8,128)(2,1)}) custom-call(s32[5]{0:T(128)} %stack.36.place_ref, bf16[768,1024]{1,0:T(8,128)(2,1)} %pad_maximum_fusion.2.refs_0_, bf16[768,1024]{1,0:T(8,128)(2,1)} %collective-permute-done.14.refs_1_, bf16[768,1024]{1,0:T(8,128)(2,1)} %copy-done.29, ...), custom_call_target="tpu_custom_call" | custom-call | flops 25769803776 | bytes 67108864 | tf_op jit(solution)/shard_map/pallas_call | solution.py:150
  592.1 32.0 %collective-permute-done.18 = f32[192,2048]{1,0:T(8,128)} collective-permute-done((f32[192,2048]{1,0:T(8,128)}, f32[192,2048]{1,0:T(8,128)}, u32[]{:S(2)}, u32[]{:S(2)}) %collective-permute-start.18) | collective-permute-done | bytes 1572896 | tf_op jit(solution)/shard_map/ppermute | solution.py:237
  628.3 55.6 %shard_map.157 = bf16[1536,1792]{1,0:T(8,128)(2,1)} custom-call(bf16[768,4096]{1,0:T(8,128)(2,1)} %get-tuple-element.79.mine_ref, bf16[768,4096]{1,0:T(8,128)(2,1)} %collective-permute-done.19.other_ref, bf16[4096,1792]{1,0:T(8,128)(2,1)} %gate_ref.9, bf16[4096,1792]{1,0:T(8,128)(2,1)} %up_ref.9), custom_call_target="tpu_custom_call" | custom-call | flops 45097156608 | bytes 25165824 | tf_op jit(solution)/shard_map/pallas_call | solution.py:189
  683.9 16.3 %collective-permute-done.20 = f32[768,2048]{1,0:T(8,128)} collective-permute-done((f32[768,2048]{1,0:T(8,128)}, f32[768,2048]{1,0:T(8,128)}, u32[]{:S(2)}, u32[]{:S(2)}) %collective-permute-start.20) | collective-permute-done | bytes 6291488 | tf_op jit(solution)/shard_map/ppermute | solution.py:237
  705.6 15.9 %convolution_convert_fusion.3 = bf16[1536,2048]{1,0:T(8,128)(2,1)} fusion(bf16[1536,1792]{1,0:T(8,128)(2,1)S(1)} %copy-done.30, bf16[1792,4096]{1,0:T(8,128)(2,1)} %param.21, s32[]{:T(128)S(6)} %select_n.196), kind=kOutput, calls=%fused_computation.3 | convolution fusion | flops 11277434880 | bytes 19136516 | tf_op jit(solution)/shard_map/dot_general | solution.py:323
  739.7 33.5 %collective-permute-done.23.refs_1_ = bf16[768,1024]{1,0:T(8,128)(2,1)} collective-permute-done((bf16[768,1024]{1,0:T(8,128)(2,1)S(1)}, bf16[768,1024]{1,0:T(8,128)(2,1)}, u32[]{:S(2)}, u32[]{:S(2)}) %collective-permute-start.23) | collective-permute-done | bytes 1572896 | tf_op jit(solution)/shard_map/ppermute | solution.py:237
  778.0 15.6 %convolution_convert_fusion.2 = bf16[1536,2048]{1,0:T(8,128)(2,1)S(1)} fusion(bf16[1536,1792]{1,0:T(8,128)(2,1)} %shard_map.157, bf16[1792,4096]{1,0:T(8,128)(2,1)} %param.21, s32[]{:T(128)S(6)} %select_n.197), kind=kOutput, calls=%fused_computation.2 | convolution fusion | flops 11277434880 | bytes 19136516 | tf_op jit(solution)/shard_map/dot_general | solution.py:325
  802.8 40.6 %shard_map.159 = (bf16[768,4096]{1,0:T(8,128)(2,1)}, bf16[768,4096]{1,0:T(8,128)(2,1)}) custom-call(s32[5]{0:T(128)} %stack.36.place_ref, bf16[768,1024]{1,0:T(8,128)(2,1)} %copy-done.19, bf16[768,1024]{1,0:T(8,128)(2,1)} %collective-permute-done.23.refs_1_, bf16[768,1024]{1,0:T(8,128)(2,1)} %copy-done.27, ...), custom_call_target="tpu_custom_call" | custom-call | flops 25769803776 | bytes 67108864 | tf_op jit(solution)/shard_map/pallas_call | solution.py:150
  855.2 57.2 %shard_map.160 = bf16[1536,1792]{1,0:T(8,128)(2,1)} custom-call(bf16[768,4096]{1,0:T(8,128)(2,1)} %get-tuple-element.91.mine_ref, bf16[768,4096]{1,0:T(8,128)(2,1)} %collective-permute-done.28.other_ref, bf16[4096,1792]{1,0:T(8,128)(2,1)} %gate_ref.9, bf16[4096,1792]{1,0:T(8,128)(2,1)} %up_ref.9), custom_call_target="tpu_custom_call" | custom-call | flops 45097156608 | bytes 25165824 | tf_op jit(solution)/shard_map/pallas_call | solution.py:189
  912.4 61.6 %collective-permute-done.29 = f32[768,2048]{1,0:T(8,128)} collective-permute-done((f32[768,2048]{1,0:T(8,128)}, f32[768,2048]{1,0:T(8,128)}, u32[]{:S(2)}, u32[]{:S(2)}) %collective-permute-start.29) | collective-permute-done | bytes 6291488 | tf_op jit(solution)/shard_map/ppermute | solution.py:237
  979.2 14.4 %convolution_convert_fusion.1 = bf16[1536,2048]{1,0:T(8,128)(2,1)S(1)} fusion(bf16[1536,1792]{1,0:T(8,128)(2,1)S(1)} %copy-done.31, bf16[1792,4096]{1,0:T(8,128)(2,1)} %param.21, s32[]{:T(128)S(6)} %select_n.196), kind=kOutput, calls=%fused_computation.1 | convolution fusion | flops 11277434880 | bytes 19136516 | tf_op jit(solution)/shard_map/dot_general | solution.py:323
  1006.9 17.6 %collective-permute-done.32.refs_1_ = bf16[384,1024]{1,0:T(8,128)(2,1)S(1)} collective-permute-done((bf16[384,1024]{1,0:T(8,128)(2,1)S(1)}, bf16[384,1024]{1,0:T(8,128)(2,1)S(1)}, u32[]{:S(2)}, u32[]{:S(2)}) %collective-permute-start.32) | collective-permute-done | bytes 786464 | tf_op jit(solution)/shard_map/ppermute | solution.py:237
  1029.2 15.6 %convolution_convert_fusion = bf16[1536,2048]{1,0:T(8,128)(2,1)S(1)} fusion(bf16[1536,1792]{1,0:T(8,128)(2,1)} %shard_map.160, bf16[1792,4096]{1,0:T(8,128)(2,1)} %param.21, s32[]{:T(128)S(6)} %select_n.197), kind=kOutput, calls=%fused_computation | convolution fusion | flops 11277434880 | bytes 19136516 | tf_op jit(solution)/shard_map/dot_general | solution.py:325
  1052.0 24.6 %shard_map.162 = (bf16[384,4096]{1,0:T(8,128)(2,1)}, bf16[384,4096]{1,0:T(8,128)(2,1)}) custom-call(s32[5]{0:T(128)} %stack.36.place_ref, bf16[384,1024]{1,0:T(8,128)(2,1)} %copy-done.14, bf16[384,1024]{1,0:T(8,128)(2,1)} %copy-done.22, bf16[384,1024]{1,0:T(8,128)(2,1)} %copy-done.23, bf16[384,1024]{1,0:T(8,128)(2,1)} %collective-permute-done.34.refs_3_, ...), custom_call_target="tpu_custom_call" | custom-call | flops 12884901888 | bytes 67108864 | tf_op jit(solution)/shard_map/pallas_call | solution.py:150
  1091.2 34.4 %shard_map.163 = bf16[768,1792]{1,0:T(8,128)(2,1)} custom-call(bf16[384,4096]{1,0:T(8,128)(2,1)} %get-tuple-element.102.mine_ref, bf16[384,4096]{1,0:T(8,128)(2,1)} %collective-permute-done.38.other_ref, bf16[4096,1792]{1,0:T(8,128)(2,1)} %gate_ref.9, bf16[4096,1792]{1,0:T(8,128)(2,1)} %up_ref.9), custom_call_target="tpu_custom_call" | custom-call | flops 22548578304 | bytes 12582912 | tf_op jit(solution)/shard_map/pallas_call | solution.py:189
  1125.6 80.1 %collective-permute-done.39 = f32[768,2048]{1,0:T(8,128)} collective-permute-done((f32[768,2048]{1,0:T(8,128)}, f32[768,2048]{1,0:T(8,128)}, u32[]{:S(2)}, u32[]{:S(2)}) %collective-permute-start.39) | collective-permute-done | bytes 6291488 | tf_op jit(solution)/shard_map/ppermute | solution.py:237
  1231.1 23.8 %collective-permute-done.44 = f32[384,2048]{1,0:T(8,128)S(1)} collective-permute-done((f32[384,2048]{1,0:T(8,128)S(1)}, f32[384,2048]{1,0:T(8,128)S(1)}, u32[]{:S(2)}, u32[]{:S(2)}) %collective-permute-start.44) | collective-permute-done | bytes 3145760 | tf_op jit(solution)/shard_map/ppermute | solution.py:237
  1262.5 79.4 %collective-permute-done.41 = f32[384,2048]{1,0:T(8,128)S(1)} collective-permute-done((f32[384,2048]{1,0:T(8,128)}, f32[384,2048]{1,0:T(8,128)S(1)}, u32[]{:S(2)}, u32[]{:S(2)}) %collective-permute-start.41) | collective-permute-done | bytes 3145760 | tf_op jit(solution)/shard_map/ppermute | solution.py:237
  1346.1 18.5 %collective-permute-done.42 = f32[192,2048]{1,0:T(8,128)S(1)} collective-permute-done((f32[192,2048]{1,0:T(8,128)S(1)}, f32[192,2048]{1,0:T(8,128)S(1)}, u32[]{:S(2)}, u32[]{:S(2)}) %collective-permute-start.42) | collective-permute-done | bytes 1572896 | tf_op jit(solution)/shard_map/ppermute | solution.py:237
  (225 shorter events, 307.4 us)
Async XLA Ops:
  7.2 190.9 %all-gather.12.cloned.1.call-start = ((), (), s32[]{:S(2)}) async-start(), calls=%async_computation | async-start | bytes 37748736 | tf_op jit(solution)/shard_map/all_gather | solution.py:251
  12.9 1356.9 %all-gather.22.cloned.1.call-start = ((), (), s32[]{:S(2)}) async-start(), calls=%async_computation.5 | async-start | bytes 7077888 | tf_op jit(solution)/shard_map/all_gather | solution.py:310
  101.0 37.6 %collective-permute-start.1 = (bf16[384,1024]{1,0:T(8,128)(2,1)S(1)}, bf16[384,1024]{1,0:T(8,128)(2,1)S(1)}, u32[]{:S(2)}, u32[]{:S(2)}) collective-permute-start(bf16[384,1024]{1,0:T(8,128)(2,1)S(1)} %pad_maximum_fusion.4.refs_0_), channel_id=1, source_target_pairs={{0,2},{1,5},{2,0},{3,7},{4,6},{5,1},{6,4},{7,3},{8,10},{9,13},{10,... | collective-permute-start | bytes 2359304 | tf_op jit(solution)/shard_map/ppermute | solution.py:237
  103.6 38.6 %collective-permute-start.2 = (bf16[384,1024]{1,0:T(8,128)(2,1)S(1)}, bf16[384,1024]{1,0:T(8,128)(2,1)}, u32[]{:S(2)}, u32[]{:S(2)}) collective-permute-start(bf16[384,1024]{1,0:T(8,128)(2,1)S(1)} %pad_maximum_fusion.4.refs_0_), channel_id=1, source_target_pairs={{0,4},{1,3},{2,6},{3,1},{4,0},{5,7},{6,2},{7,5},{8,12},{9,11},{10,... | collective-permute-start | bytes 2359304 | tf_op jit(solution)/shard_map/ppermute | solution.py:237
  237.1 44.3 %collective-permute-start.6 = (bf16[768,512]{1,0:T(8,128)(2,1)}, bf16[768,512]{1,0:T(8,128)(2,1)}, u32[]{:S(2)}, u32[]{:S(2)}) collective-permute-start(bf16[768,512]{1,0:T(8,128)(2,1)} %get-tuple-element.65), channel_id=1, source_target_pairs={{0,1},{1,0},{2,3},{3,2},{4,5},{5,4},{6,7},{7,6},{8,9},{9,8},{10,11... | collective-permute-start | bytes 2359304 | tf_op jit(solution)/shard_map/ppermute | solution.py:237
  281.1 49.2 %collective-permute-start.5 = (bf16[768,2048]{1,0:T(8,128)(2,1)}, bf16[768,2048]{1,0:T(8,128)(2,1)}, u32[]{:S(2)}, u32[]{:S(2)}) collective-permute-start(bf16[768,2048]{1,0:T(8,128)(2,1)} %fusion.14), channel_id=1, source_target_pairs={{0,1},{1,0},{2,3},{3,2},{4,5},{5,4},{6,7},{7,6},{8,9},{9,8},{10,11... | collective-permute-start | bytes 9437192 | tf_op jit(solution)/shard_map/ppermute | solution.py:237
  283.9 36.9 %collective-permute-start.7 = (bf16[768,1024]{1,0:T(8,128)(2,1)}, bf16[768,1024]{1,0:T(8,128)(2,1)}, u32[]{:S(2)}, u32[]{:S(2)}) collective-permute-start(bf16[768,1024]{1,0:T(8,128)(2,1)} %pad_maximum_fusion.1.refs_0_), channel_id=1, source_target_pairs={{0,2},{1,5},{2,0},{3,7},{4,6},{5,1},{6,4},{7,3},{8,10},{9,13},{10,... | collective-permute-start | bytes 4718600 | tf_op jit(solution)/shard_map/ppermute | solution.py:237
  285.3 49.9 %collective-permute-start.8 = (bf16[768,1024]{1,0:T(8,128)(2,1)}, bf16[768,1024]{1,0:T(8,128)(2,1)S(1)}, u32[]{:S(2)}, u32[]{:S(2)}) collective-permute-start(bf16[768,1024]{1,0:T(8,128)(2,1)} %pad_maximum_fusion.1.refs_0_), channel_id=1, source_target_pairs={{0,4},{1,3},{2,6},{3,1},{4,0},{5,7},{6,2},{7,5},{8,12},{9,11},{10,... | collective-permute-start | bytes 4718600 | tf_op jit(solution)/shard_map/ppermute | solution.py:237
  381.8 66.0 %collective-permute-start.11 = (f32[384,2048]{1,0:T(8,128)}, f32[384,2048]{1,0:T(8,128)}, u32[]{:S(2)}, u32[]{:S(2)}) collective-permute-start(f32[384,2048]{1,0:T(8,128)} %convert_add_fusion.4), channel_id=1, source_target_pairs={{0,2},{1,5},{2,0},{3,7},{4,6},{5,1},{6,4},{7,3},{8,10},{9,13},{10,... | collective-permute-start | bytes 9437192 | tf_op jit(solution)/shard_map/ppermute | solution.py:237
  468.5 68.6 %collective-permute-start.12 = (bf16[1536,2048]{1,0:T(8,128)(2,1)}, bf16[1536,2048]{1,0:T(8,128)(2,1)}, u32[]{:S(2)}, u32[]{:S(2)}) collective-permute-start(bf16[1536,2048]{1,0:T(8,128)(2,1)} %convolution_convert_fusion.5), channel_id=1, source_target_pairs={{0,1},{1,0},{2,3},{3,2},{4,5},{5,4},{6,7},{7,6},{8,9},{9,8},{10,11... | collective-permute-start | bytes 18874376 | tf_op jit(solution)/shard_map/ppermute | solution.py:237
  484.3 37.2 %collective-permute-start.14 = (bf16[768,1024]{1,0:T(8,128)(2,1)}, bf16[768,1024]{1,0:T(8,128)(2,1)}, u32[]{:S(2)}, u32[]{:S(2)}) collective-permute-start(bf16[768,1024]{1,0:T(8,128)(2,1)} %pad_maximum_fusion.2.refs_0_), channel_id=1, source_target_pairs={{0,2},{1,5},{2,0},{3,7},{4,6},{5,1},{6,4},{7,3},{8,10},{9,13},{10,... | collective-permute-start | bytes 4718600 | tf_op jit(solution)/shard_map/ppermute | solution.py:237
  485.9 59.2 %collective-permute-start.15 = (bf16[768,1024]{1,0:T(8,128)(2,1)}, bf16[768,1024]{1,0:T(8,128)(2,1)S(1)}, u32[]{:S(2)}, u32[]{:S(2)}) collective-permute-start(bf16[768,1024]{1,0:T(8,128)(2,1)} %pad_maximum_fusion.2.refs_0_), channel_id=1, source_target_pairs={{0,4},{1,3},{2,6},{3,1},{4,0},{5,7},{6,2},{7,5},{8,12},{9,11},{10,... | collective-permute-start | bytes 4718600 | tf_op jit(solution)/shard_map/ppermute | solution.py:237
  587.0 41.3 %collective-permute-start.19 = (bf16[768,4096]{1,0:T(8,128)(2,1)}, bf16[768,4096]{1,0:T(8,128)(2,1)}, u32[]{:S(2)}, u32[]{:S(2)}) collective-permute-start(bf16[768,4096]{1,0:T(8,128)(2,1)} %get-tuple-element.79.mine_ref), channel_id=1, source_target_pairs={{0,1},{1,0},{2,3},{3,2},{4,5},{5,4},{6,7},{7,6},{8,9},{9,8},{10,11... | collective-permute-start | bytes 18874376 | tf_op jit(solution)/shard_map/ppermute | solution.py:237
  587.4 36.7 %collective-permute-start.18 = (f32[192,2048]{1,0:T(8,128)}, f32[192,2048]{1,0:T(8,128)}, u32[]{:S(2)}, u32[]{:S(2)}) collective-permute-start(f32[192,2048]{1,0:T(8,128)} %dynamic-slice_add_fusion.4), channel_id=1, source_target_pairs={{0,4},{1,3},{2,6},{3,1},{4,0},{5,7},{6,2},{7,5},{8,12},{9,11},{10,... | collective-permute-start | bytes 4718600 | tf_op jit(solution)/shard_map/ppermute | solution.py:237
  589.1 111.1 %collective-permute-start.20 = (f32[768,2048]{1,0:T(8,128)}, f32[768,2048]{1,0:T(8,128)}, u32[]{:S(2)}, u32[]{:S(2)}) collective-permute-start(f32[768,2048]{1,0:T(8,128)} %convert_add_fusion.2), channel_id=1, source_target_pairs={{0,2},{1,5},{2,0},{3,7},{4,6},{5,1},{6,4},{7,3},{8,10},{9,13},{10,... | collective-permute-start | bytes 18874376 | tf_op jit(solution)/shard_map/ppermute | solution.py:237
  628.3 749.4 %all-gather.20.cloned.1.call-start = ((), (), s32[]{:S(2)}) async-start(), calls=%async_computation.4 | async-start | bytes 14155776 | tf_op jit(solution)/shard_map/all_gather | solution.py:310
  721.5 72.1 %collective-permute-start.21 = (bf16[1536,2048]{1,0:T(8,128)(2,1)}, bf16[1536,2048]{1,0:T(8,128)(2,1)}, u32[]{:S(2)}, u32[]{:S(2)}) collective-permute-start(bf16[1536,2048]{1,0:T(8,128)(2,1)} %convolution_convert_fusion.3), channel_id=1, source_target_pairs={{0,1},{1,0},{2,3},{3,2},{4,5},{5,4},{6,7},{7,6},{8,9},{9,8},{10,11... | collective-permute-start | bytes 18874376 | tf_op jit(solution)/shard_map/ppermute | solution.py:237
  736.5 36.8 %collective-permute-start.23 = (bf16[768,1024]{1,0:T(8,128)(2,1)S(1)}, bf16[768,1024]{1,0:T(8,128)(2,1)}, u32[]{:S(2)}, u32[]{:S(2)}) collective-permute-start(bf16[768,1024]{1,0:T(8,128)(2,1)S(1)} %pad_maximum_fusion.3.refs_0_), channel_id=1, source_target_pairs={{0,2},{1,5},{2,0},{3,7},{4,6},{5,1},{6,4},{7,3},{8,10},{9,13},{10,... | collective-permute-start | bytes 4718600 | tf_op jit(solution)/shard_map/ppermute | solution.py:237
  738.0 63.7 %collective-permute-start.24 = (bf16[768,1024]{1,0:T(8,128)(2,1)S(1)}, bf16[768,1024]{1,0:T(8,128)(2,1)S(1)}, u32[]{:S(2)}, u32[]{:S(2)}) collective-permute-start(bf16[768,1024]{1,0:T(8,128)(2,1)S(1)} %pad_maximum_fusion.3.refs_0_), channel_id=1, source_target_pairs={{0,4},{1,3},{2,6},{3,1},{4,0},{5,7},{6,2},{7,5},{8,12},{9,11},{10,... | collective-permute-start | bytes 4718600 | tf_op jit(solution)/shard_map/ppermute | solution.py:237
  777.6 67.4 %collective-permute-start.26 = (bf16[384,2048]{1,0:T(8,128)(2,1)}, bf16[384,2048]{1,0:T(8,128)(2,1)}, u32[]{:S(2)}, u32[]{:S(2)}) collective-permute-start(bf16[384,2048]{1,0:T(8,128)(2,1)} %dynamic_slice.190), channel_id=1, source_target_pairs={{0,1},{1,0},{2,3},{3,2},{4,5},{5,4},{6,7},{7,6},{8,9},{9,8},{10,11... | collective-permute-start | bytes 4718600 | tf_op jit(solution)/shard_map/ppermute | solution.py:237
  777.6 67.4 %collective-permute-start.27 = (f32[384,2048]{1,0:T(8,128)}, f32[384,2048]{1,0:T(8,128)}, u32[]{:S(2)}, u32[]{:S(2)}) collective-permute-start(f32[384,2048]{1,0:T(8,128)} %dynamic-slice_add_fusion.2), channel_id=1, source_target_pairs={{0,4},{1,3},{2,6},{3,1},{4,0},{5,7},{6,2},{7,5},{8,12},{9,11},{10,... | collective-permute-start | bytes 9437192 | tf_op jit(solution)/shard_map/ppermute | solution.py:237
  852.0 537.0 %all-gather.18.cloned.1.call-start = ((), (), s32[]{:S(2)}) async-start(), calls=%async_computation.3 | async-start | bytes 14155776 | tf_op jit(solution)/shard_map/all_gather | solution.py:310
  852.1 121.9 %collective-permute-start.29 = (f32[768,2048]{1,0:T(8,128)}, f32[768,2048]{1,0:T(8,128)}, u32[]{:S(2)}, u32[]{:S(2)}) collective-permute-start(f32[768,2048]{1,0:T(8,128)} %convert_add_fusion.1), channel_id=1, source_target_pairs={{0,2},{1,5},{2,0},{3,7},{4,6},{5,1},{6,4},{7,3},{8,10},{9,13},{10,... | collective-permute-start | bytes 18874376 | tf_op jit(solution)/shard_map/ppermute | solution.py:237
  993.7 51.1 %collective-permute-start.30 = (bf16[1536,2048]{1,0:T(8,128)(2,1)S(1)}, bf16[1536,2048]{1,0:T(8,128)(2,1)S(1)}, u32[]{:S(2)}, u32[]{:S(2)}) collective-permute-start(bf16[1536,2048]{1,0:T(8,128)(2,1)S(1)} %convolution_convert_fusion.1), channel_id=1, source_target_pairs={{0,1},{1,0},{2,3},{3,2},{4,5},{5,4},{6,7},{7,6},{8,9},{9,8},{10,11... | collective-permute-start | bytes 18874376 | tf_op jit(solution)/shard_map/ppermute | solution.py:237
  1005.4 45.8 %collective-permute-start.33 = (bf16[384,1024]{1,0:T(8,128)(2,1)S(1)}, bf16[384,1024]{1,0:T(8,128)(2,1)S(1)}, u32[]{:S(2)}, u32[]{:S(2)}) collective-permute-start(bf16[384,1024]{1,0:T(8,128)(2,1)S(1)} %pad_maximum_fusion.5.refs_0_), channel_id=1, source_target_pairs={{0,4},{1,3},{2,6},{3,1},{4,0},{5,7},{6,2},{7,5},{8,12},{9,11},{10,... | collective-permute-start | bytes 2359304 | tf_op jit(solution)/shard_map/ppermute | solution.py:237
  1027.5 49.2 %collective-permute-start.36 = (bf16[384,2048]{1,0:T(8,128)(2,1)}, bf16[384,2048]{1,0:T(8,128)(2,1)}, u32[]{:S(2)}, u32[]{:S(2)}) collective-permute-start(bf16[384,2048]{1,0:T(8,128)(2,1)} %dynamic_slice.204), channel_id=1, source_target_pairs={{0,1},{1,0},{2,3},{3,2},{4,5},{5,4},{6,7},{7,6},{8,9},{9,8},{10,11... | collective-permute-start | bytes 4718600 | tf_op jit(solution)/shard_map/ppermute | solution.py:237
  1027.5 49.2 %collective-permute-start.37 = (f32[384,2048]{1,0:T(8,128)}, f32[384,2048]{1,0:T(8,128)}, u32[]{:S(2)}, u32[]{:S(2)}) collective-permute-start(f32[384,2048]{1,0:T(8,128)} %dynamic-slice_add_fusion.1), channel_id=1, source_target_pairs={{0,4},{1,3},{2,6},{3,1},{4,0},{5,7},{6,2},{7,5},{8,12},{9,11},{10,... | collective-permute-start | bytes 9437192 | tf_op jit(solution)/shard_map/ppermute | solution.py:237
  1083.7 316.8 %all-gather.16.cloned.1.call-start = ((), (), s32[]{:S(2)}) async-start(), calls=%async_computation.2 | async-start | bytes 14155776 | tf_op jit(solution)/shard_map/all_gather | solution.py:310
  1083.8 121.9 %collective-permute-start.39 = (f32[768,2048]{1,0:T(8,128)}, f32[768,2048]{1,0:T(8,128)}, u32[]{:S(2)}, u32[]{:S(2)}) collective-permute-start(f32[768,2048]{1,0:T(8,128)} %convert_add_fusion), channel_id=1, source_target_pairs={{0,2},{1,5},{2,0},{3,7},{4,6},{5,1},{6,4},{7,3},{8,10},{9,13},{10,... | collective-permute-start | bytes 18874376 | tf_op jit(solution)/shard_map/ppermute | solution.py:237
  1217.7 37.3 %collective-permute-start.44 = (f32[384,2048]{1,0:T(8,128)S(1)}, f32[384,2048]{1,0:T(8,128)S(1)}, u32[]{:S(2)}, u32[]{:S(2)}) collective-permute-start(f32[384,2048]{1,0:T(8,128)S(1)} %dynamic-slice_add_fusion), channel_id=1, source_target_pairs={{0,4},{1,3},{2,6},{3,1},{4,0},{5,7},{6,2},{7,5},{8,12},{9,11},{10,... | collective-permute-start | bytes 9437192 | tf_op jit(solution)/shard_map/ppermute | solution.py:237
  1260.7 151.2 %all-gather.14.cloned.1.call-start = ((), (), s32[]{:S(2)}) async-start(), calls=%async_computation.1 | async-start | bytes 7077888 | tf_op jit(solution)/shard_map/all_gather | solution.py:310
  1261.1 80.8 %collective-permute-start.41 = (f32[384,2048]{1,0:T(8,128)}, f32[384,2048]{1,0:T(8,128)S(1)}, u32[]{:S(2)}, u32[]{:S(2)}) collective-permute-start(f32[384,2048]{1,0:T(8,128)} %convert_add_fusion.3), channel_id=1, source_target_pairs={{0,2},{1,5},{2,0},{3,7},{4,6},{5,1},{6,4},{7,3},{8,10},{9,13},{10,... | collective-permute-start | bytes 9437192 | tf_op jit(solution)/shard_map/ppermute | solution.py:237
  (54 other events, 1066.7 us)
Sparse Core Ops, SparseCore 0:
  13.0 185.0 all-gather.11
  628.4 57.0 all-gather.21
  852.1 94.0 all-gather.19
  1083.9 94.9 all-gather.17
  1260.8 94.1 all-gather.15
  1367.7 44.0 all-gather.13
